TPU v7x, 32 devices: a whole 2x2x4 slice. The times are simulated.
32 devices in a mesh: slides: 2 (over y), seq: 4 (over z), sub: 4 (over x, core).
Axes of the slice: x: 2, y: 2, z: 4, core: 2. Of those that a mesh axis runs over, the one named last changes fastest.
Arguments:
- q_heads: bfloat16 [8192, 768], P(('slides', 'seq'), 'sub'), parts along dimension 0, may hold values from -8 to 8
- k_heads: bfloat16 [8192, 768], P(('slides', 'seq'), 'sub'), parts along dimension 0, may hold values from -8 to 8
- v_heads: bfloat16 [8192, 768], P(('slides', 'seq'), 'sub'), parts along dimension 0, may hold values from -6 to 6
- w_out: bfloat16 [768, 768], replicated, may hold values from -0.21875 to 0.21875
- offsets: int32 [2, 16], replicated, may hold values from 0 to 15, as said below
- valid: int32 [2], P('slides'), parts along dimension 0, may hold values from 3073 to 4096
Outputs:
- mixed: bfloat16 [8192, 768], P(('slides', 'seq'), 'sub'), parts along dimension 0
There are 2 independent parts, one for each index of `slides`. A program takes and returns all parts, laid end to end along the dimension named above; an argument that names none is the same for every part. Nothing has to cross between parts.
Inputs may be any that keep to these rules, and one draw needn't show every extreme that they name: `offsets`: row 0 lies below 4, row 1 below 16. Tiles at positions valid[0] and beyond are padding.
All inputs are finite; a program needn't handle non-finite values.
Results may differ from a plain program's by a relative error of at most 0.012.
Values may be sent and summed in bfloat16 or wider, within the bound.
A program may use at most 64 MiB of HBM per device.

v0:
```python
import functools

import jax
import jax.numpy as jnp
from jax import lax
from jax.experimental import pallas as pl
from jax.experimental.pallas import tpu as pltpu
from jax.sharding import PartitionSpec as P

HS = 48
GROUP = 4
R1 = 4
R2 = 16
LANES = 128
HALF = 64
MASKED = -1e30
MESH = pl.DeviceIdType.MESH
EXP_SCALE = HS ** (-0.5) * 1.4426950408889634


def pick(masks, parts):
    out = parts[-1]
    for mask, part in zip(masks[:-1], parts[:-1]):
        out = jnp.where(mask, part, out)
    return out


def kernel(
    n_seq, n_sub, heads,
    q_hbm, k_hbm, v_hbm, w_hbm, off_ref, valid_ref, o_ref,
    q_ref, k_ref, v_ref, w_ref,
    qp, kx, vx, qw, wide, mid, wk, wv, mk, mv,
    st_m, st_l, st_a, xg, xw, wl, wr, so, at_x,
    wide_send, wide_recv, mid_send, mid_recv, x_send, x_recv, in_sem,
):
    rows = q_ref.shape[1]
    cols = heads * HS
    phase = rows // R1
    strip = rows // R2
    subs = R2 // R1
    half_rows = phase // 2
    seq = lax.axis_index("seq")
    sub = lax.axis_index("sub")
    pos = lax.rem(seq, GROUP)
    group0 = seq - pos
    limit = valid_ref[0]
    has_left = pos > 0
    has_right = pos < GROUP - 1
    bits = [1 << b for b in reversed(range(n_sub.bit_length() - 1))]

    fetches = [
        pltpu.make_async_copy(src, dst, in_sem.at[i])
        for i, (src, dst) in enumerate(
            ((k_hbm, k_ref), (v_hbm, v_ref), (q_hbm, q_ref), (w_hbm, w_ref))
        )
    ]
    for fetch in fetches:
        fetch.start()
    barrier = pltpu.get_barrier_semaphore()
    for step in (1, n_seq - 1):
        pl.semaphore_signal(
            barrier, inc=1, device_id={"seq": lax.rem(seq + step, n_seq)}, device_id_type=MESH
        )
    for bit in bits:
        pl.semaphore_signal(barrier, inc=1, device_id={"sub": sub ^ bit}, device_id_type=MESH)

    lane = lax.broadcasted_iota(jnp.int32, (1, LANES), 1)
    low = lane < HALF

    def off_lanes(which, first_head, base, tile):
        at = lane + tile * LANES - base
        out = jnp.zeros((1, LANES), jnp.int32)
        for h in range(heads):
            here = ((at >= h * HS) & (at < (h + 1) * HS)) | (at == cols + h)
            out = jnp.where(here, off_ref[which, first_head + h], out)
        return out

    def head_mask(h, base, tiles=2):
        at = lax.broadcasted_iota(jnp.int32, (1, tiles * LANES), 1) - base
        here = (at >= h * HS) & (at < (h + 1) * HS)
        if base == 0:
            here = here | (at == cols + h)
        return here

    mine = sub * heads
    left_off = [[off_lanes(b, mine, 0, t) for t in range(2)] for b in range(2)]
    right_off = [[off_lanes(b, mine, HALF, t) for t in range(2)] for b in range(2)]
    kv_off = [
        [left_off[b][0], jnp.where(low, left_off[b][1], right_off[b][0]), right_off[b][1]]
        for b in range(2)
    ]

    square = R2 * R2
    at_row = lax.broadcasted_iota(jnp.int32, (square, square), 0)
    at_tok = lax.broadcasted_iota(jnp.int32, (square, square), 1)
    one_hot = jnp.where(at_tok == at_row % R2 * R2 + at_row // R2, 1.0, 0.0).astype(jnp.bfloat16)
    contract_last = (((1,), (1,)), ((), ()))
    contract_first = (((0,), (0,)), ((), ()))

    turned = [[lax.rem(off + s, R1) for off in left_off[0]] for s in range(R1)]
    row64 = lax.broadcasted_iota(jnp.int32, (strip, LANES), 0) * R2
    row16 = lax.broadcasted_iota(jnp.int32, (R2, LANES), 0) * R2
    block0 = seq * rows
    with jax.named_scope("load"):
        for fetch in fetches[:3]:
            fetch.wait()
        for blk in range(rows // square):
            toks = pl.ds(blk * square, square)
            kv_t = jnp.concatenate([k_ref[:, toks], v_ref[:, toks]], axis=0)
            q_t = jnp.concatenate([q_ref[:, toks], jnp.ones((HALF, square), jnp.bfloat16)], axis=0)
            kv = lax.dot_general(one_hot, kv_t, contract_last, preferred_element_type=jnp.float32)
            qs = lax.dot_general(one_hot, q_t, contract_last, preferred_element_type=jnp.float32)
            wide_kv = [None] * 3
            wide_q = [None] * 2
            for a in range(subs):
                mid_kv = [None] * 3
                slab_q = [[None] * 2 for _ in range(R1)]
                for m in range(R1):
                    j = a * R1 + m
                    to = pl.ds(m * phase + a * strip + blk * R2, R2)
                    kv_j, q_j = kv[j * R2:(j + 1) * R2], qs[j * R2:(j + 1) * R2]
                    tiles = [kv_j[:, i * LANES:(i + 1) * LANES] for i in range(3)]
                    q_tiles = [q_j[:, i * LANES:(i + 1) * LANES] for i in range(2)]
                    dead = jnp.where(block0 + blk * square + row16 + j < limit, 0.0, MASKED)
                    kx[to, :LANES] = tiles[0].astype(jnp.bfloat16)
                    kx[to, LANES:] = jnp.where(low, tiles[1], dead).astype(jnp.bfloat16)
                    vx[to, :LANES] = jnp.where(low, 1.0, tiles[1]).astype(jnp.bfloat16)
                    vx[to, LANES:] = tiles[2].astype(jnp.bfloat16)
                    for i, tile in enumerate(tiles):
                        mid_kv[i] = tile if m == 0 else jnp.where(kv_off[0][i] == m, tile, mid_kv[i])
                        wide_kv[i] = tile if j == 0 else jnp.where(kv_off[1][i] == j, tile, wide_kv[i])
                    for i, tile in enumerate(q_tiles):
                        for s in range(R1):
                            here = turned[s][i] == m
                            slab_q[s][i] = tile if m == 0 else jnp.where(here, tile, slab_q[s][i])
                        wide_q[i] = tile if j == 0 else jnp.where(left_off[1][i] == j, tile, wide_q[i])
                to = pl.ds((a % 2) * strip + blk * R2, R2)
                for i in range(3):
                    mid[pos, a // 2, to, i * LANES:(i + 1) * LANES] = mid_kv[i].astype(jnp.bfloat16)
                for s in range(R1):
                    to = pl.ds(s * phase + a * strip + blk * R2, R2)
                    for i in range(2):
                        qp[to, i * LANES:(i + 1) * LANES] = slab_q[s][i].astype(jnp.bfloat16)
            to = pl.ds(blk * R2, R2)
            for i in range(3):
                wide[seq, to, i * LANES:(i + 1) * LANES] = wide_kv[i].astype(jnp.bfloat16)
            for i in range(2):
                qw[to, i * LANES:(i + 1) * LANES] = wide_q[i].astype(jnp.bfloat16)

    with jax.named_scope("barrier"):
        pl.semaphore_wait(barrier, 2 + len(bits))

    def wide_copy(origin, rightward):
        target = seq + 1 if rightward else seq - 1
        return pltpu.make_async_remote_copy(
            src_ref=wide.at[origin], dst_ref=wide.at[origin],
            send_sem=wide_send.at[0 if rightward else 1, origin], recv_sem=wide_recv.at[origin],
            device_id={"seq": target}, device_id_type=MESH,
        )

    @pl.when(seq < n_seq - 1)
    def _():
        wide_copy(seq, True).start()

    @pl.when(seq > 0)
    def _():
        wide_copy(seq, False).start()

    def wide_relay(dist):
        @pl.when(seq - dist >= 0)
        def _():
            wide_copy(seq - dist, True).wait_recv()

            @pl.when(seq < n_seq - 1)
            def _():
                wide_copy(seq - dist, True).start()

        @pl.when(seq + dist < n_seq)
        def _():
            wide_copy(seq + dist, False).wait_recv()

            @pl.when(seq > 0)
            def _():
                wide_copy(seq + dist, False).start()

    def mid_copy(origin, chunk, rightward):
        way = 0 if rightward else 1
        target = seq + 1 if rightward else seq - 1
        return pltpu.make_async_remote_copy(
            src_ref=mid.at[origin, chunk], dst_ref=mid.at[origin, chunk],
            send_sem=mid_send.at[way, origin, chunk], recv_sem=mid_recv.at[origin, chunk],
            device_id={"seq": target}, device_id_type=MESH,
        )

    for chunk in range(2):
        @pl.when(has_right)
        def _():
            mid_copy(pos, chunk, True).start()

        @pl.when(has_left)
        def _():
            mid_copy(pos, chunk, False).start()

    def relay(dist, chunk):
        @pl.when(pos - dist >= 0)
        def _():
            mid_copy(pos - dist, chunk, True).wait_recv()

            @pl.when(has_right)
            def _():
                mid_copy(pos - dist, chunk, True).start()

        @pl.when(pos + dist < GROUP)
        def _():
            mid_copy(pos + dist, chunk, False).wait_recv()

            @pl.when(has_left)
            def _():
                mid_copy(pos + dist, chunk, False).start()

    with jax.named_scope("weights"):
        fetches[3].wait()
        for d in range(n_sub):
            wl[pl.ds(d * 2 * LANES + cols, HALF), :] = jnp.zeros((HALF, cols), jnp.bfloat16)
            wr[pl.ds(d * 2 * LANES, HALF), :] = jnp.zeros((HALF, cols), jnp.bfloat16)
        for s in range(n_sub):
            @pl.when(sub == s)
            def _():
                for d in range(n_sub):
                    part = w_ref[d * cols:(d + 1) * cols, s * cols:(s + 1) * cols]
                    wl[pl.ds(d * 2 * LANES, cols), :] = part
                    wr[pl.ds(d * 2 * LANES + HALF, cols), :] = part

    def attend(q_blk, keys, values, h, before=None):
        masked_q = jnp.where(head_mask(h, 0), q_blk.astype(jnp.float32), 0.0).astype(jnp.bfloat16)
        scores = lax.dot_general(masked_q, keys, contract_last, preferred_element_type=jnp.float32)
        peak = jnp.max(scores, axis=1, keepdims=True)
        if before is not None:
            peak = jnp.maximum(peak, before)
        probs = jnp.exp2((scores - peak) * EXP_SCALE).astype(jnp.bfloat16)
        return peak, jnp.dot(probs, values, preferred_element_type=jnp.float32)

    def pack(slab, value):
        dst = xw.at[sub] if slab is None else xg.at[sub, slab]
        top_half, bot = value[:value.shape[0] // 2], value[value.shape[0] // 2:]
        moved = pltpu.roll(top_half, LANES + HALF, 1)
        dst[:, :LANES] = moved[:, :LANES].astype(jnp.bfloat16)
        dst[:, LANES:2 * LANES] = jnp.where(
            low, moved[:, LANES:], bot[:, :LANES]
        ).astype(jnp.bfloat16)
        dst[:, 2 * LANES:] = bot[:, LANES:].astype(jnp.bfloat16)

    def x_ref(block, slab):
        return xw.at[block] if isinstance(slab, int) and slab == R1 else xg.at[block, slab]

    def x_copy(at_bit, held, slab):
        bit = bits[at_bit]
        ref = x_ref(sub ^ held, slab)
        return pltpu.make_async_remote_copy(
            src_ref=ref, dst_ref=ref,
            send_sem=x_send.at[at_bit, held, slab], recv_sem=x_recv.at[held ^ bit, slab],
            device_id={"sub": sub ^ bit}, device_id_type=MESH,
        )

    def x_plan():
        held, plan = [0], []
        for at_bit, bit in enumerate(bits):
            plan += [(at_bit, x) for x in held]
            held = held + [x ^ bit for x in held]
        return plan

    def x_start(slab):
        for at_bit, x in x_plan():
            if x == 0:
                x_copy(at_bit, x, slab).start()

    def x_recv_wait(block, slab):
        ref = x_ref(sub ^ block, slab)
        pltpu.make_async_remote_copy(
            src_ref=ref, dst_ref=ref,
            send_sem=x_send.at[0, 0, slab], recv_sem=x_recv.at[block, slab],
            device_id={"sub": sub ^ block}, device_id_type=MESH,
        ).wait_recv()

    def x_forward(slab):
        waited = set()
        for at_bit, x in x_plan():
            if x:
                if x not in waited:
                    waited.add(x)
                    x_recv_wait(x, slab)
                x_copy(at_bit, x, slab).start()
        return waited

    def x_finish(slab, waited):
        for x in range(1, n_sub):
            if x not in waited:
                x_recv_wait(x, slab)

    def near_step(it, carry):
        slab = lax.rem(it + 1, R1)
        at = pl.ds(pl.multiple_of(slab * phase, phase), phase)
        q_blk = qp[at, :]
        acc = top = mass = None
        for h in range(heads):
            peak, out = attend(q_blk, kx[...], vx[...], h)
            here = head_mask(h, HALF)
            total = out[:, 0:1]
            shape = out.shape
            if h == 0:
                acc, top, mass = out, jnp.broadcast_to(peak, shape), jnp.broadcast_to(total, shape)
            else:
                acc = jnp.where(here, out, acc)
                top = jnp.where(here, peak, top)
                mass = jnp.where(here, total, mass)
        st_a[at, :] = acc
        st_m[at, :] = top
        st_l[at, :] = mass

        @pl.when(it < R1 - 1)
        def _():
            pack(slab, acc / mass)
            x_start(slab)

        @pl.when(it == 1)
        def _():
            wide_relay(1)
            relay(1, 0)

        @pl.when(it == 2)
        def _():
            wide_relay(2)
            relay(1, 1)
            x_forward(1)

        @pl.when(it == 3)
        def _():
            for dist in range(3, n_seq):
                wide_relay(dist)
            relay(2, 0)
            x_forward(2)

        return carry

    with jax.named_scope("near"):
        lax.fori_loop(0, R1, near_step, 0)

    def merge(q_blk, keys, values, top, mass, acc):
        for h in range(heads):
            here = head_mask(h, HALF)
            before = jnp.max(jnp.where(here, top, -3e38), axis=1, keepdims=True)
            peak, out = attend(q_blk, keys, values, h, before)
            fade = jnp.exp2((before - peak) * EXP_SCALE)
            total = out[:, 0:1]
            acc = jnp.where(here, acc * fade + out, acc)
            mass = jnp.where(here, mass * fade + total, mass)
            top = jnp.where(here, peak, top)
        return top, mass, acc

    mid_lane_off = left_off[0][1]
    pair_row = lax.broadcasted_iota(jnp.int32, (half_rows, LANES), 0)
    pair_row = (pair_row % strip) * R2 + (pair_row // strip) * R1
    pair = GROUP // 2
    own_pair = lax.div(pos, pair)

    def mid_merge(which):
        for o in range(pair):
            origin = which * pair + o
            for chunk in range(2):
                to = pl.ds(o * phase + chunk * half_rows, half_rows)
                tile1 = mid[origin, chunk, :, LANES:2 * LANES].astype(jnp.float32)
                place = (group0 + origin) * rows + pair_row + (chunk * 2 * R1 + mid_lane_off)
                dead = jnp.where(place < limit, 0.0, MASKED)
                mk[to, :LANES] = mid[origin, chunk, :, :LANES]
                mk[to, LANES:] = jnp.where(low, tile1, dead).astype(jnp.bfloat16)
                mv[to, :LANES] = jnp.where(low, 1.0, tile1).astype(jnp.bfloat16)
                mv[to, LANES:] = mid[origin, chunk, :, 2 * LANES:]
        at = pl.ds(0, phase)
        return merge(qp[at, :], mk[...], mv[...], st_m[at, :], st_l[at, :], st_a[at, :])

    with jax.named_scope("mid_merge_own"):
        for ref, new in zip((st_m, st_l, st_a), mid_merge(own_pair)):
            ref[pl.ds(0, phase), :] = new
        relay(2, 1)
        x_forward(3)

    r_off = [jnp.concatenate(right_off[b], axis=1) for b in range(2)]
    wide_lane_off = left_off[1][1]
    for o in range(n_seq):
        at = pl.ds(o * strip, strip)
        tile1 = wide[o, :, LANES:2 * LANES].astype(jnp.float32)
        dead = jnp.where(o * rows + row64 + wide_lane_off < limit, 0.0, MASKED)
        wk[at, :LANES] = wide[o, :, :LANES]
        wk[at, LANES:] = jnp.where(low, tile1, dead).astype(jnp.bfloat16)
        wv[at, :LANES] = jnp.where(low, 1.0, tile1).astype(jnp.bfloat16)
        wv[at, LANES:] = wide[o, :, 2 * LANES:]

    with jax.named_scope("wide_merge"):
        slab_of = lax.rem(r_off[1] + R1 - r_off[0], R1)
        part_of = lax.div(r_off[1], R1)
        strip_of = slab_of * subs + part_of
        wide_masks = [strip_of == j for j in range(R2)]
        state = [
            pick(wide_masks, [ref[pl.ds(j * strip, strip), :] for j in range(R2)])
            for ref in (st_m, st_l, st_a)
        ]
        state = merge(qw[...], wk[...], wv[...], *state)
        for ref, new in zip((st_m, st_l, st_a), state):
            for j in range(subs):
                at = pl.ds(j * strip, strip)
                ref[at, :] = jnp.where(wide_masks[j], new, ref[at, :])
        wide_out = state[2] / state[1]
    with jax.named_scope("relays"):
        for chunk in range(2):
            relay(3, chunk)

    with jax.named_scope("mid_merge"):
        state = mid_merge(1 - own_pair)
        mid_out = state[2] / state[1]
        pack(0, mid_out)
        x_start(0)
        parts = [mid_out[a * strip:(a + 1) * strip] for a in range(subs)]
        shared = pick([part_of == a for a in range(subs)], parts)
        pack(None, jnp.where(slab_of == 0, shared, wide_out))
        x_start(R1)
    with jax.named_scope("x_wait"):
        relayed = {x for at_bit, x in x_plan() if x}
        done = {slab: relayed for slab in range(1, R1)}
        for slab in (0, R1):
            done[slab] = x_forward(slab)
        for slab in (1, 2, 3, 0, R1):
            x_finish(slab, done[slab])

    with jax.named_scope("project"):
        for d in range(n_sub):
            offs, wide_offs = [
                [
                    jnp.concatenate([off_lanes(b, d * heads, base, t) for t in range(2)], axis=1)
                    for base in (0, HALF)
                ]
                for b in range(2)
            ]
            first = xw[d, :, :2 * LANES].astype(jnp.float32)
            second = xw[d, :, LANES:].astype(jnp.float32)
            wide_rows = [
                jnp.concatenate([first, pltpu.roll(second, LANES + HALF, 1)], axis=0),
                jnp.concatenate([pltpu.roll(first, HALF, 1), second], axis=0),
            ]
            for half in range(2):
                take = slice(half * LANES, half * LANES + 2 * LANES)
                slabs = [xg[d, i, :, take].astype(jnp.float32) for i in range(R1)]
                spare = wide_rows[half]
                for m in range(R1):
                    masks = [offs[half] == (m - i) % R1 for i in range(R1)]
                    rows_m = pick(masks, slabs)
                    rows_m = jnp.concatenate(
                        [
                            jnp.where(
                                wide_offs[half] == (half * 2 + i) * R1 + m, spare,
                                rows_m[i * strip:(i + 1) * strip],
                            )
                            for i in range(2)
                        ],
                        axis=0,
                    )
                    at_x[half, pl.ds(m * half_rows, half_rows), pl.ds(d * 2 * LANES, 2 * LANES)] = (
                        rows_m.astype(jnp.bfloat16)
                    )
        for half in range(2):
            out = jnp.dot(at_x[half], (wl, wr)[half][...], preferred_element_type=jnp.float32)
            out = out.astype(jnp.bfloat16)
            for m in range(R1):
                to = pl.ds(m * phase + half * half_rows, half_rows)
                so[to, :] = out[m * half_rows:(m + 1) * half_rows]
        for blk in range(rows // square):
            picked = jnp.concatenate(
                [
                    so[pl.ds((j % R1) * phase + (j // R1) * strip + blk * R2, R2), :]
                    for j in range(R2)
                ],
                axis=0,
            )
            res = lax.dot_general(picked, one_hot, contract_first, preferred_element_type=jnp.float32)
            place = block0 + blk * square + lax.broadcasted_iota(jnp.int32, (1, square), 1)
            o_ref[:, pl.ds(blk * square, square)] = jnp.where(place < limit, res, 0.0).astype(jnp.bfloat16)

    with jax.named_scope("drain"):
        for o in range(n_seq):
            @pl.when((seq < n_seq - 1) & (seq >= o))
            def _():
                wide_copy(o, True).wait_send()

            @pl.when((seq > 0) & (seq <= o))
            def _():
                wide_copy(o, False).wait_send()
        for chunk in range(2):
            for o in range(GROUP):
                @pl.when(has_right & (pos >= o))
                def _():
                    mid_copy(o, chunk, True).wait_send()

                @pl.when(has_left & (pos <= o))
                def _():
                    mid_copy(o, chunk, False).wait_send()
        for slab in range(R1 + 1):
            for at_bit, x in x_plan():
                x_copy(at_bit, x, slab).wait_send()


def local(n_seq, n_sub, q_heads, k_heads, v_heads, w_out, offsets, valid):
    rows, cols = q_heads.shape
    heads = cols // HS
    phase, strip = rows // R1, rows // R2
    bf, f32 = jnp.bfloat16, jnp.float32
    n_bits = n_sub.bit_length() - 1
    assert cols == LANES + HALF and n_sub == 1 << n_bits
    vmem = pl.BlockSpec(memory_space=pltpu.VMEM)
    smem = pl.BlockSpec(memory_space=pltpu.SMEM)
    wide_all = n_seq * strip
    return pl.pallas_call(
        functools.partial(kernel, n_seq, n_sub, heads),
        out_shape=jax.ShapeDtypeStruct((cols, rows), bf),
        in_specs=[pl.BlockSpec(memory_space=pl.ANY)] * 4 + [smem] * 2,
        out_specs=vmem,
        scratch_shapes=[
            pltpu.VMEM((cols, rows), bf),
            pltpu.VMEM((cols, rows), bf),
            pltpu.VMEM((cols, rows), bf),
            pltpu.VMEM(w_out.shape, bf),
            pltpu.VMEM((rows, 2 * LANES), bf),
            pltpu.VMEM((rows, 2 * LANES), bf),
            pltpu.VMEM((rows, 2 * LANES), bf),
            pltpu.VMEM((strip, 2 * LANES), bf),
            pltpu.VMEM((n_seq, strip, 3 * LANES), bf),
            pltpu.VMEM((GROUP, 2, phase // 2, 3 * LANES), bf),
            pltpu.VMEM((wide_all, 2 * LANES), bf),
            pltpu.VMEM((wide_all, 2 * LANES), bf),
            pltpu.VMEM((GROUP // 2 * phase, 2 * LANES), bf),
            pltpu.VMEM((GROUP // 2 * phase, 2 * LANES), bf),
            pltpu.VMEM((rows, 2 * LANES), f32),
            pltpu.VMEM((rows, 2 * LANES), f32),
            pltpu.VMEM((rows, 2 * LANES), f32),
            pltpu.VMEM((n_sub, R1, phase // 2, 3 * LANES), bf),
            pltpu.VMEM((n_sub, strip // 2, 3 * LANES), bf),
            pltpu.VMEM((n_sub * 2 * LANES, cols), bf),
            pltpu.VMEM((n_sub * 2 * LANES, cols), bf),
            pltpu.VMEM((rows, cols), bf),
            pltpu.VMEM((2, rows // 2, n_sub * 2 * LANES), bf),
            pltpu.SemaphoreType.DMA((2, n_seq)),
            pltpu.SemaphoreType.DMA((n_seq,)),
            pltpu.SemaphoreType.DMA((2, GROUP, 2)),
            pltpu.SemaphoreType.DMA((GROUP, 2)),
            pltpu.SemaphoreType.DMA((n_bits, n_sub, R1 + 1)),
            pltpu.SemaphoreType.DMA((n_sub, R1 + 1)),
            pltpu.SemaphoreType.DMA((4,)),
        ],
        compiler_params=pltpu.CompilerParams(
            collective_id=0, has_side_effects=True, vmem_limit_bytes=56 * 1024 * 1024
        ),
    )(q_heads.T, k_heads.T, v_heads.T, w_out, offsets, valid).T


def solution(mesh):
    spread = P(("slides", "seq"), "sub")
    return jax.shard_map(
        functools.partial(local, mesh.shape["seq"], mesh.shape["sub"]),
        mesh=mesh,
        in_specs=(spread, spread, spread, P(), P(), P("slides")),
        out_specs=spread,
        check_vma=False,
    )
```

profile of v0, /device:TPU:1, one launch (start us, length us, event | category | flops | bytes accessed | tf_op | source)
XLA Modules:
  0.0 34.4 jit_solution(17596649658536940630)
XLA Ops:
  0.7 31.9 %shard_map.64 = bf16[192,1024]{1,0:T(8,128)(2,1)} custom-call(bf16[192,1024]{1,0:T(8,128)(2,1)} %bitcast.5, bf16[192,1024]{1,0:T(8,128)(2,1)} %bitcast.6, bf16[192,1024]{1,0:T(8,128)(2,1)} %bitcast.7, bf16[768,768]{1,0:T(8,128)(2,1)} %w_hbm.1, s32[2,16]{1,0:T(2,128)} %off_ref.1, s32[1]{0:T(128)S(6)} %copy.8.valid_ref), custom_call_target="tpu_custom_call" | custom-call | tf_op jit(solution)/shard_map/pallas_call | solution.py:520
  32.6 1.8 %copy.9 = bf16[1024,192]{0,1:T(8,128)(2,1)} copy(bf16[1024,192]{0,1:T(8,128)(2,1)} %bitcast.4) | data formatting | bytes 786432
where the time goes:
time: 34.6 us; the launch traced here: 34.4 us
  Pallas kernels  31.9 us (92%)
  local copies, waits for them, and re-layouts  1.77 us (5%)
  between operations  0.66 us (2%)
    pallas_call x1, Pallas kernels, local(): pl.pallas_call(functools.partial(kernel, n_seq, n_sub, heads), out_shape=...  31.9 us
    unnamed x1, local copies, waits for them, and re-layouts  1.77 us

commit v1 on v0

v1 whole, which is shorter than its diff:
```python
import functools

import jax
import jax.numpy as jnp
from jax import lax
from jax.experimental import pallas as pl
from jax.experimental.pallas import tpu as pltpu
from jax.sharding import PartitionSpec as P

HS = 48
FP = 64
GROUP = 4
R1 = 4
R2 = 16
LANES = 128
HALF = 64
MASKED = -1e30
MESH = pl.DeviceIdType.MESH
EXP_SCALE = HS ** (-0.5) * 1.4426950408889634
LOG2E = 1.4426950408889634
CONTRACT_LAST = (((1,), (1,)), ((), ()))
BF, F32, I32 = jnp.bfloat16, jnp.float32, jnp.int32


def iota(shape, dim):
    return lax.broadcasted_iota(I32, shape, dim)


def mm(a, b):
    return jnp.dot(a, b, preferred_element_type=F32)


def mm_t(a, b):
    return lax.dot_general(a, b, CONTRACT_LAST, preferred_element_type=F32)


def combine(parts):
    top = functools.reduce(jnp.maximum, [lse for _, lse in parts])
    weights = [jnp.exp2(lse - top) for _, lse in parts]
    scale = 1.0 / functools.reduce(jnp.add, weights)
    return functools.reduce(jnp.add, [o * (w * scale) for (o, _), w in zip(parts, weights)])


def kernel(
    n_seq, n_sub, heads,
    q_hbm, k_hbm, v_hbm, w_hbm, off_hbm, valid_hbm, o_ref,
    off_ref, valid_ref,
    q_ref, k_aug, v_aug, w_ref, wt,
    perm, sel, kr, pq, pk, pv, wide, mid,
    scores, near_o, near_l, mid_o, mid_m, spread, xg,
    wide_send, wide_recv, mid_send, mid_recv, x_send, x_recv, in_sem,
):
    cols, rows = q_ref.shape
    phase = rows // R1
    strip = rows // R2
    square = 2 * LANES
    seq = lax.axis_index("seq")
    sub = lax.axis_index("sub")
    pos = lax.rem(seq, GROUP)
    group0 = seq - pos
    has_left = pos > 0
    has_right = pos < GROUP - 1
    bits = [1 << b for b in reversed(range(n_sub.bit_length() - 1))]

    small = [
        pltpu.make_async_copy(off_hbm, off_ref, in_sem.at[2 * heads + 2]),
        pltpu.make_async_copy(valid_hbm, valid_ref, in_sem.at[2 * heads + 3]),
    ]
    fetches = []
    for src, dst in ((k_hbm, k_aug), (v_hbm, v_aug)):
        for h in range(heads):
            fetches.append((src.at[pl.ds(h * HS, HS), :], dst.at[pl.ds(h * FP, HS), :]))
    fetches += [(q_hbm, q_ref), (w_hbm, w_ref)]
    fetches = [
        pltpu.make_async_copy(src, dst, in_sem.at[i]) for i, (src, dst) in enumerate(fetches)
    ]
    for fetch in small + fetches:
        fetch.start()
    barrier = pltpu.get_barrier_semaphore()
    for step, there in ((1, seq < n_seq - 1), (-1, seq > 0)):
        @pl.when(there)
        def _():
            pl.semaphore_signal(
                barrier, inc=1, device_id={"seq": seq + step}, device_id_type=MESH
            )
    for bit in bits:
        pl.semaphore_signal(barrier, inc=1, device_id={"sub": sub ^ bit}, device_id_type=MESH)

    low = iota((1, LANES), 1) < HALF
    block0 = seq * rows

    def plan(head):
        o0, o1 = off_ref[0, head], off_ref[1, head]
        m1 = lax.rem(o1, R1)
        late = o0
        second = jnp.where(m1 == o0, lax.rem(o0 + 1, R1), m1)
        third = 0
        for m in reversed(range(R1 - 1)):
            third = jnp.where((late != m) & (second != m), m, third)
        return o0, m1, lax.div(o1, R1), (late, second, third, 6 - late - second - third)

    with jax.named_scope("consts"):
        tok, at = iota((square, square), 0), iota((square, square), 1)
        for odd in range(2):
            hit = tok == at % HALF * R1 + ((at // HALF) ^ odd)
            perm[odd] = jnp.where(hit, 1.0, 0.0).astype(BF)
        at_l, at_j = iota((square, LANES), 0), iota((square, LANES), 1)
        for a in range(R1):
            for half in range(2):
                hit = at_l == (at_j - half * HALF) * R1 + a
                sel[a, pl.ds(half * square, square), :] = jnp.where(hit, 1.0, 0.0).astype(BF)
        for fetch in small:
            fetch.wait()
        limit = valid_ref[0]
        plans = [plan(sub * heads + h) for h in range(heads)]
        tail_one = jnp.where(iota((FP - HS, square), 0) == 0, 1.0, 0.0).astype(BF)
        for h in range(heads):
            tail = pl.ds(h * FP + HS, FP - HS)
            for m in range(R1):
                pq[m, tail, :] = tail_one
            place = block0 + iota((FP - HS, rows), 1)
            first = iota((FP - HS, rows), 0) == 0
            v_aug[tail, :] = jnp.where(first, 1.0, 0.0).astype(BF)
            k_aug[tail, :] = jnp.where(first & (place >= limit), MASKED, 0.0).astype(BF)

    def permuted(lhs_of, store):
        for c in range(rows // (2 * square)):
            outs = [
                mm(lhs_of(pl.ds((2 * c + b) * square, square)), perm[b]) for b in range(2)
            ]
            for m in range(R1):
                half = slice((m // 2) * LANES, (m // 2 + 1) * LANES)
                even, odd = outs[0][:, half], outs[1][:, half]
                if m % 2:
                    even, odd = odd, even
                store(m, slice(c * LANES, (c + 1) * LANES), jnp.where(low, even, odd).astype(BF))

    with jax.named_scope("load"):
        for fetch in fetches[:2 * heads]:
            fetch.wait()

        def store_kv(m, lanes, val):
            pk[m, :, lanes] = val[:cols]
            pv[m, :, lanes] = val[cols:]

        permuted(
            lambda t: jnp.concatenate(
                [ref[pl.ds(h * FP, HS), t] for ref in (k_aug, v_aug) for h in range(heads)], axis=0
            ),
            store_kv,
        )
        for h in range(heads):
            o0, m1, a, _ = plans[h]
            feat = pl.ds(h * HS, HS)
            mid[pos, h // 2, pl.ds((h % 2) * 2 * HS, HS), :] = pk[o0, feat, :]
            mid[pos, h // 2, pl.ds((h % 2) * 2 * HS + HS, HS), :] = pv[o0, feat, :]
            both = jnp.concatenate([pk[m1, feat, :], pv[m1, feat, :]], axis=1)
            wide[seq, feat, :] = mm(both, sel[a]).astype(BF)

    with jax.named_scope("barrier"):
        inner = (seq > 0) & (seq < n_seq - 1)

        @pl.when(inner)
        def _():
            pl.semaphore_wait(barrier, len(bits) + 2)

        @pl.when(jnp.logical_not(inner))
        def _():
            pl.semaphore_wait(barrier, len(bits) + 1)

    def wide_copy(origin, rightward):
        target = seq + 1 if rightward else seq - 1
        return pltpu.make_async_remote_copy(
            src_ref=wide.at[origin], dst_ref=wide.at[origin],
            send_sem=wide_send.at[0 if rightward else 1, origin], recv_sem=wide_recv.at[origin],
            device_id={"seq": target}, device_id_type=MESH,
        )

    @pl.when(seq < n_seq - 1)
    def _():
        wide_copy(seq, True).start()

    @pl.when(seq > 0)
    def _():
        wide_copy(seq, False).start()

    def wide_relay(dist):
        @pl.when(seq - dist >= 0)
        def _():
            wide_copy(seq - dist, True).wait_recv()

            @pl.when(seq < n_seq - 1)
            def _():
                wide_copy(seq - dist, True).start()

        @pl.when(seq + dist < n_seq)
        def _():
            wide_copy(seq + dist, False).wait_recv()

            @pl.when(seq > 0)
            def _():
                wide_copy(seq + dist, False).start()

    def mid_copy(origin, chunk, rightward):
        way = 0 if rightward else 1
        target = seq + 1 if rightward else seq - 1
        return pltpu.make_async_remote_copy(
            src_ref=mid.at[origin, chunk], dst_ref=mid.at[origin, chunk],
            send_sem=mid_send.at[way, origin, chunk], recv_sem=mid_recv.at[origin, chunk],
            device_id={"seq": target}, device_id_type=MESH,
        )

    @pl.when(has_right)
    def _():
        mid_copy(pos, 0, True).start()

    @pl.when(has_left)
    def _():
        mid_copy(pos, 0, False).start()

    def relay(dist, chunk):
        @pl.when(pos - dist >= 0)
        def _():
            mid_copy(pos - dist, chunk, True).wait_recv()

            @pl.when(has_right)
            def _():
                mid_copy(pos - dist, chunk, True).start()

        @pl.when(pos + dist < GROUP)
        def _():
            mid_copy(pos + dist, chunk, False).wait_recv()

            @pl.when(has_left)
            def _():
                mid_copy(pos + dist, chunk, False).start()

    def x_ref(block, slab):
        if slab in (0, R1):
            return xg.at[block, 0, pl.ds((slab // R1) * (cols // 2), cols // 2)]
        return xg.at[block, slab]

    def x_copy(at_bit, held, slab):
        bit = bits[at_bit]
        ref = x_ref(sub ^ held, slab)
        return pltpu.make_async_remote_copy(
            src_ref=ref, dst_ref=ref,
            send_sem=x_send.at[at_bit, held, slab], recv_sem=x_recv.at[held ^ bit, slab],
            device_id={"sub": sub ^ bit}, device_id_type=MESH,
        )

    def x_plan():
        held, todo = [0], []
        for at_bit, bit in enumerate(bits):
            todo += [(at_bit, x) for x in held]
            held = held + [x ^ bit for x in held]
        return todo

    def x_start(slab):
        for at_bit, x in x_plan():
            if x == 0:
                x_copy(at_bit, x, slab).start()

    def x_recv_wait(block, slab):
        ref = x_ref(sub ^ block, slab)
        pltpu.make_async_remote_copy(
            src_ref=ref, dst_ref=ref,
            send_sem=x_send.at[0, 0, slab], recv_sem=x_recv.at[block, slab],
            device_id={"sub": sub ^ block}, device_id_type=MESH,
        ).wait_recv()

    def x_forward(slab):
        waited = set()
        for at_bit, x in x_plan():
            if x:
                if x not in waited:
                    waited.add(x)
                    x_recv_wait(x, slab)
                x_copy(at_bit, x, slab).start()
        return waited

    with jax.named_scope("prep"):
        fetches[2 * heads].wait()

        def store_q(m, lanes, val):
            for h in range(heads):
                pq[m, pl.ds(h * FP, HS), lanes] = val[h * HS:(h + 1) * HS]

        permuted(lambda t: q_ref[:, t], store_q)
        for h in range(heads):
            kr[h] = k_aug[pl.ds(h * FP, FP), :].T

    def attend(keys, values, queries, before=None):
        scores = mm(keys, queries)
        peak = jnp.max(scores, axis=0, keepdims=True)
        if before is not None:
            peak = jnp.maximum(peak, before)
        probs = jnp.exp2((scores - peak) * EXP_SCALE).astype(BF)
        return peak, mm(values, probs)

    def finish(peak, out):
        mass = out[HS:HS + 1]
        return out[:HS] * (1.0 / mass), peak * EXP_SCALE + jnp.log(mass) * LOG2E

    pieces = rows // phase

    def score_piece(to, h, m, c, peak):
        keys = kr[h, pl.ds(c * phase, phase), :]
        part = mm(keys, pq[m, pl.ds(h * FP, FP), :])
        scores[to, pl.ds(c * phase, phase), :] = part
        top = jnp.max(part, axis=0, keepdims=True)
        return top if peak is None else jnp.maximum(peak, top)

    combos = [(m, h) for m in range(R1) for h in range(heads)]

    def mid_start(chunk):
        @pl.when(has_right)
        def _():
            mid_copy(pos, chunk, True).start()

        @pl.when(has_left)
        def _():
            mid_copy(pos, chunk, False).start()

    def near_step(i, peak):
        m, h = combos[i]
        ahead = acc = None
        for c in range(pieces):
            if i + 1 < len(combos):
                m_next, h_next = combos[i + 1]
                ahead = score_piece((i + 1) % 2, h_next, m_next, c, ahead)
            part = scores[i % 2, pl.ds(c * phase, phase), :]
            probs = jnp.exp2((part - peak) * EXP_SCALE).astype(BF)
            out = mm(v_aug[pl.ds(h * FP, FP), pl.ds(c * phase, phase)], probs)
            acc = out if acc is None else acc + out
        out, lse = finish(peak, acc)
        near_o[m, pl.ds(h * HS, HS), :] = out
        near_l[m, pl.ds(h, 1), :] = lse
        return ahead

    with jax.named_scope("near"):
        peak = None
        for c in range(pieces):
            peak = score_piece(0, 0, 0, c, peak)
        for i in range(len(combos)):
            peak = near_step(i, peak)
            if i == 6:
                wide_relay(1)
                mid_start(1)
            if i == 12:
                relay(1, 0)

    def ship(slab, h, val):
        xg[sub, slab, pl.ds(h * HS, HS), :] = val.astype(BF)

    with jax.named_scope("ship_near"):
        for slab in (2, 3):
            for h in range(heads):
                ship(slab, h, near_o[plans[h][3][slab], pl.ds(h * HS, HS), :])
            x_start(slab)

    ones_tail = jnp.where(iota((FP - HS, phase), 0) == 0, 1.0, 0.0).astype(BF)

    def mid_step(origin, chunk, first):
        pair = range(chunk * 2, chunk * 2 + 2)
        lane = iota((FP - HS, phase), 1)
        top_row = iota((FP - HS, phase), 0) == 0
        scored, vals, fore = [], [], []
        for h in pair:
            o0 = plans[h][0]
            at = jnp.where(lax.rem(o0, 2) == 1, lane ^ HALF, lane)
            place = (group0 + origin) * rows + at * R1 + o0
            dead = jnp.where(top_row & (place >= limit), MASKED, 0.0).astype(BF)
            k_at, v_at = [pl.ds((h % 2) * 2 * HS + i * HS, HS) for i in range(2)]
            k_t = jnp.concatenate([mid[origin, chunk, k_at, :], dead], axis=0)
            vals.append(jnp.concatenate([mid[origin, chunk, v_at, :], ones_tail], axis=0))
            scored.append(mm(k_t.T, pq[o0, pl.ds(h * FP, FP), :]))
            fore.append(None if first else (mid_m[pl.ds(h, 1), :], mid_o[pl.ds(h * FP, FP), :]))
        done = []
        for score, val, before in zip(scored, vals, fore):
            peak = jnp.max(score, axis=0, keepdims=True)
            if before is not None:
                peak = jnp.maximum(peak, before[0])
            probs = jnp.exp2((score - peak) * EXP_SCALE).astype(BF)
            done.append((peak, mm(val, probs)))
        for i, h in enumerate(pair):
            peak, out = done[i]
            if not first:
                out = out + fore[i][1] * jnp.exp2((fore[i][0] - peak) * EXP_SCALE)
            done[i] = (peak, out)
            mid_m[pl.ds(h, 1), :] = peak
            mid_o[pl.ds(h * FP, FP), :] = out
        return done

    partner = pos ^ 1
    second = 2 - lax.div(pos, 2)
    third = 3 - 3 * lax.div(pos, 2)

    with jax.named_scope("mid_own"):
        mid_step(pos, 0, True)
    with jax.named_scope("wide_relay2"):
        wide_relay(2)
    with jax.named_scope("mid_1"):
        mid_step(pos, 1, True)
        mid_step(partner, 0, False)
    with jax.named_scope("relay11"):
        relay(1, 1)
    with jax.named_scope("mid_1b"):
        mid_step(partner, 1, False)
    with jax.named_scope("weights"):
        fetches[2 * heads + 1].wait()
        for s in range(n_sub):
            @pl.when(sub == s)
            def _():
                wt[...] = w_ref[:, s * cols:(s + 1) * cols].T
    with jax.named_scope("relay20"):
        relay(2, 0)
    with jax.named_scope("mid_2"):
        mid_step(second, 0, False)
    with jax.named_scope("x_fwd2"):
        waited = {2: x_forward(2)}
    with jax.named_scope("wide_relay3"):
        for dist in range(3, n_seq):
            wide_relay(dist)

    with jax.named_scope("wide"):
        q_rows = []
        for h in range(heads):
            _, m1, a, _ = plans[h]
            q_h = mm(pq[m1, pl.ds(h * FP, FP), :], sel[a, pl.ds((h % 2) * square, square), :])
            zero = jnp.zeros((FP, LANES), BF)
            q_h = q_h.astype(BF)
            q_rows.append(jnp.concatenate([q_h, zero] if h < 2 else [zero, q_h], axis=1))
        q_wide = jnp.concatenate(q_rows, axis=0)
        keys, values = [], []
        zeros_tail = jnp.zeros((FP - HS - 8, LANES), F32)
        for pr in range(n_seq // 2):
            one, two = [wide[2 * pr + i].astype(F32) for i in range(2)]
            k_pair = jnp.where(low, one, pltpu.roll(two, HALF, 1))
            v_pair = jnp.where(low, pltpu.roll(one, HALF, 1), two)
            k_rows, v_rows = [], []
            for h in range(heads):
                _, m1, a, _ = plans[h]
                lane = iota((FP - HS, LANES), 1)
                row0 = iota((FP - HS, LANES), 0) == 0
                at = lane % HALF * R1 + a
                at = jnp.where(lax.rem(m1, 2) == 1, at ^ HALF, at)
                place = (2 * pr + lane // HALF) * rows + at * R1 + m1
                k_rows += [
                    k_pair[h * HS:(h + 1) * HS],
                    jnp.where(row0 & (place >= limit), MASKED, 0.0),
                ]
                v_rows += [v_pair[h * HS:(h + 1) * HS], jnp.where(row0, 1.0, 0.0)]
            keys.append(jnp.concatenate(k_rows, axis=0).astype(BF).T)
            values.append(jnp.concatenate(v_rows, axis=0).astype(BF))
        peak, out = attend(
            jnp.concatenate(keys, axis=0), jnp.concatenate(values, axis=1), q_wide
        )
        for h in range(heads):
            _, m1, a, _ = plans[h]
            col = slice((h // 2) * LANES, (h // 2 + 1) * LANES)
            o_h, lse = finish(peak[:, col], out[h * FP:(h + 1) * FP, col])
            top = jnp.floor(lse * 0.25) * 4.0
            rest = lse - top
            middle = jnp.floor(rest * 64.0) * (1.0 / 64.0)
            r = iota((FP - HS, LANES), 0)
            tail = jnp.where(r == 0, top, jnp.where(r == 1, middle, jnp.where(r == 2, rest - middle, jnp.where(r == 3, 1.0, 0.0))))
            z = jnp.concatenate([o_h, tail], axis=0).astype(BF)
            put = mm_t(z, sel[a, pl.ds((h % 2) * square, square), :])
            spread[pl.ds(h * FP, HS), :] = put[:HS]
            lse = put[HS:HS + 1] + put[HS + 1:HS + 2] + put[HS + 2:HS + 3]
            lse = jnp.where(put[HS + 3:HS + 4] > 0.5, lse, MASKED)
            spread[pl.ds(h * FP + HS, 8), :] = jnp.broadcast_to(lse, (8, phase))
            two = plans[h][3][1]
            feat = pl.ds(h * HS, HS)
            lse = jnp.where(two == m1, lse, MASKED)
            ship(1, h, combine([
                (near_o[two, feat, :], near_l[two, pl.ds(h, 1), :]), (put[:HS], lse),
            ]))
        x_start(1)

    with jax.named_scope("relay21"):
        relay(2, 1)
    with jax.named_scope("mid_2b"):
        mid_step(second, 1, False)
    with jax.named_scope("x_fwd3"):
        waited[3] = x_forward(3)

    for chunk in range(2):
        with jax.named_scope("relay3"):
            relay(3, chunk)
        with jax.named_scope("mid_3"):
            done = mid_step(third, chunk, False)
            for h in range(chunk * 2, chunk * 2 + 2):
                o0, m1 = plans[h][:2]
                feat = pl.ds(h * HS, HS)
                lse_w = spread[pl.ds(h * FP + HS, 1), :]
                ship(0, h, combine([
                    (near_o[o0, feat, :], near_l[o0, pl.ds(h, 1), :]),
                    finish(*done[h % 2]),
                    (spread[pl.ds(h * FP, HS), :], jnp.where(m1 == o0, lse_w, MASKED)),
                ]))
            x_start(chunk * R1)
        if chunk == 0:
            with jax.named_scope("x_fwd1"):
                waited[1] = x_forward(1)

    with jax.named_scope("x_wait"):
        for slab in (0, R1):
            waited[slab] = x_forward(slab)
        for slab in (2, 3, 1, 0, R1):
            for x in range(1, n_sub):
                if x not in waited[slab]:
                    x_recv_wait(x, slab)

    with jax.named_scope("project"):
        outs = []
        every = [plan(i)[3] for i in range(n_sub * heads)]
        for m in range(R1):
            parts = []
            for d in range(n_sub):
                for h in range(heads):
                    order = every[d * heads + h]
                    slab = 3
                    for s in range(3):
                        slab = jnp.where(order[s] == m, s, slab)
                    parts.append(xg[d, slab, pl.ds(h * HS, HS), :])
            outs.append(mm(wt[...], jnp.concatenate(parts, axis=0)).astype(BF).astype(F32))
        for c in range(rows // (2 * square)):
            at = slice(c * LANES, (c + 1) * LANES)
            for odd in range(2):
                pieces = [
                    jnp.where(low, outs[2 * i + odd][:, at], outs[2 * i + 1 - odd][:, at])
                    for i in range(2)
                ]
                res = mm_t(jnp.concatenate(pieces, axis=1).astype(BF), perm[odd])
                first = (2 * c + odd) * square
                place = block0 + first + iota((1, square), 1)
                o_ref[:, first:first + square] = jnp.where(place < limit, res, 0.0).astype(BF)

    with jax.named_scope("drain"):
        for o in range(n_seq):
            @pl.when((seq < n_seq - 1) & (seq >= o))
            def _():
                wide_copy(o, True).wait_send()

            @pl.when((seq > 0) & (seq <= o))
            def _():
                wide_copy(o, False).wait_send()
        for chunk in range(2):
            for o in range(GROUP):
                @pl.when(has_right & (pos >= o))
                def _():
                    mid_copy(o, chunk, True).wait_send()

                @pl.when(has_left & (pos <= o))
                def _():
                    mid_copy(o, chunk, False).wait_send()
        for slab in range(R1 + 1):
            for at_bit, x in x_plan():
                x_copy(at_bit, x, slab).wait_send()


def local(n_seq, n_sub, q_heads, k_heads, v_heads, w_out, offsets, valid):
    rows, cols = q_heads.shape
    heads = cols // HS
    phase, strip = rows // R1, rows // R2
    n_bits = n_sub.bit_length() - 1
    assert heads == 4 and n_sub == 1 << n_bits and n_seq % 2 == 0 and strip == HALF
    vmem = pl.BlockSpec(memory_space=pltpu.VMEM)
    pad = heads * FP
    return pl.pallas_call(
        functools.partial(kernel, n_seq, n_sub, heads),
        out_shape=jax.ShapeDtypeStruct((cols, rows), BF),
        in_specs=[pl.BlockSpec(memory_space=pl.ANY)] * 6,
        out_specs=vmem,
        scratch_shapes=[
            pltpu.SMEM(offsets.shape, I32),
            pltpu.SMEM(valid.shape, I32),
            pltpu.VMEM((cols, rows), BF),
            pltpu.VMEM((pad, rows), BF),
            pltpu.VMEM((pad, rows), BF),
            pltpu.VMEM(w_out.shape, BF),
            pltpu.VMEM((cols, w_out.shape[0]), BF),
            pltpu.VMEM((2, 2 * LANES, 2 * LANES), BF),
            pltpu.VMEM((R1, 4 * LANES, LANES), BF),
            pltpu.VMEM((heads, rows, FP), BF),
            pltpu.VMEM((R1, pad, phase), BF),
            pltpu.VMEM((R1, cols, phase), BF),
            pltpu.VMEM((R1, cols, phase), BF),
            pltpu.VMEM((n_seq, cols, LANES), BF),
            pltpu.VMEM((GROUP, 2, cols, phase), BF),
            pltpu.VMEM((2, rows, phase), F32),
            pltpu.VMEM((R1, cols, phase), F32),
            pltpu.VMEM((R1, 8, phase), F32),
            pltpu.VMEM((pad, phase), F32),
            pltpu.VMEM((8, phase), F32),
            pltpu.VMEM((pad, phase), F32),
            pltpu.VMEM((n_sub, R1, cols, phase), BF),
            pltpu.SemaphoreType.DMA((2, n_seq)),
            pltpu.SemaphoreType.DMA((n_seq,)),
            pltpu.SemaphoreType.DMA((2, GROUP, 2)),
            pltpu.SemaphoreType.DMA((GROUP, 2)),
            pltpu.SemaphoreType.DMA((n_bits, n_sub, R1 + 1)),
            pltpu.SemaphoreType.DMA((n_sub, R1 + 1)),
            pltpu.SemaphoreType.DMA((2 * heads + 4,)),
        ],
        compiler_params=pltpu.CompilerParams(
            collective_id=0, has_side_effects=True, vmem_limit_bytes=56 * 1024 * 1024
        ),
    )(q_heads.T, k_heads.T, v_heads.T, w_out, offsets, valid).T


def solution(mesh):
    spread = P(("slides", "seq"), "sub")
    return jax.shard_map(
        functools.partial(local, mesh.shape["seq"], mesh.shape["sub"]),
        mesh=mesh,
        in_specs=(spread, spread, spread, P(), P(), P("slides")),
        out_specs=spread,
        check_vma=False,
    )
```

time: 34.6 us -> 31.6 us (0.913)
  Pallas kernels: 31.9 us -> 29 us
    pallas_call x1, Pallas kernels: 31.9 us -> 29 us  [local(): pl.pallas_call(functools.partial(kernel, n_seq, n_sub, heads), out_shape=...]
where the time goes in v1:
time: 31.6 us; the launch traced here: 31.4 us
  Pallas kernels  29 us (92%)
  local copies, waits for them, and re-layouts  1.77 us (6%)
  between operations  0.66 us (2%)
    pallas_call x1, Pallas kernels, local(): pl.pallas_call(functools.partial(kernel, n_seq, n_sub, heads), out_shape=...  29 us
    unnamed x1, local copies, waits for them, and re-layouts  1.77 us

profile of v1, /device:TPU:1, one launch (start us, length us, event | category | flops | bytes accessed | tf_op | source)
XLA Modules:
  0.0 31.4 jit_solution(7374334343613304987)
XLA Ops:
  0.7 29.0 %shard_map.64 = bf16[192,1024]{1,0:T(8,128)(2,1)} custom-call(bf16[192,1024]{1,0:T(8,128)(2,1)} %bitcast.5, bf16[192,1024]{1,0:T(8,128)(2,1)} %bitcast.6, bf16[192,1024]{1,0:T(8,128)(2,1)} %bitcast.7, bf16[768,768]{1,0:T(8,128)(2,1)} %w_hbm.1, s32[2,16]{1,0:T(2,128)} %off_hbm.1, s32[1]{0:T(128)S(6)} %copy.8.valid_hbm), custom_call_target="tpu_custom_call" | custom-call | tf_op jit(solution)/shard_map/pallas_call | solution.py:572
  29.6 1.8 %copy.9 = bf16[1024,192]{0,1:T(8,128)(2,1)} copy(bf16[1024,192]{0,1:T(8,128)(2,1)} %bitcast.4) | data formatting | bytes 786432

commit v2 on v1

v2 whole, which is shorter than its diff:
```python
import functools

import jax
import jax.numpy as jnp
from jax import lax
from jax.experimental import pallas as pl
from jax.experimental.pallas import tpu as pltpu
from jax.sharding import PartitionSpec as P

HS = 48
FP = 64
GROUP = 4
R1 = 4
R2 = 16
LANES = 128
HALF = 64
MASKED = -1e30
MESH = pl.DeviceIdType.MESH
EXP_SCALE = HS ** (-0.5) * 1.4426950408889634
LOG2E = 1.4426950408889634
CONTRACT_LAST = (((1,), (1,)), ((), ()))
BF, F32, I32 = jnp.bfloat16, jnp.float32, jnp.int32


def iota(shape, dim):
    return lax.broadcasted_iota(I32, shape, dim)


def mm(a, b):
    return jnp.dot(a, b, preferred_element_type=F32)


def mm_t(a, b):
    return lax.dot_general(a, b, CONTRACT_LAST, preferred_element_type=F32)


def combine(parts):
    top = functools.reduce(jnp.maximum, [lse for _, lse in parts])
    weights = [jnp.exp2(lse - top) for _, lse in parts]
    scale = 1.0 / functools.reduce(jnp.add, weights)
    return functools.reduce(jnp.add, [o * (w * scale) for (o, _), w in zip(parts, weights)])


def kernel(
    n_seq, n_sub, heads,
    q_hbm, k_hbm, v_hbm, w_hbm, off_hbm, valid_hbm, o_ref,
    off_ref, valid_ref,
    q_ref, k_aug, v_aug, w_ref, wt, wt_last,
    perm, sel, kr, pq, pk, pv, wide, mid,
    guest, mq, mkr, mv, ret, fin_o, fin_l,
    scores, near_o, near_l, mid_o, mid_m, spread, xg, xl,
    wide_send, wide_recv, mid_send, mid_recv, q_sem, ret_send, ret_recv, x_send, x_recv, in_sem,
):
    cols, rows = q_ref.shape
    phase = rows // R1
    strip = rows // R2
    square = 2 * LANES
    seq = lax.axis_index("seq")
    sub = lax.axis_index("sub")
    pos = lax.rem(seq, GROUP)
    group0 = seq - pos
    partner = pos ^ 1
    across = GROUP - 1 - pos
    far = across ^ 1
    is_host = (pos == 1) | (pos == 2)
    is_guest = jnp.logical_not(is_host)
    bits = [1 << b for b in reversed(range(n_sub.bit_length() - 1))]

    small = [
        pltpu.make_async_copy(off_hbm, off_ref, in_sem.at[4]),
        pltpu.make_async_copy(valid_hbm, valid_ref, in_sem.at[5]),
    ]
    for copy in small:
        copy.start()
    for i, (src, dst) in enumerate(((k_hbm, k_aug), (v_hbm, v_aug))):
        for h in range(heads):
            pltpu.make_async_copy(
                src.at[pl.ds(h * HS, HS), :], dst.at[pl.ds(h * FP, HS), :], in_sem.at[i]
            ).start()
    q_fetch = pltpu.make_async_copy(q_hbm, q_ref, in_sem.at[2])
    w_fetch = pltpu.make_async_copy(w_hbm, w_ref, in_sem.at[3])
    q_fetch.start()
    barrier = pltpu.get_barrier_semaphore()
    for step, there in ((1, seq < n_seq - 1), (-1, seq > 0)):
        @pl.when(there)
        def _():
            pl.semaphore_signal(
                barrier, inc=1, device_id={"seq": seq + step}, device_id_type=MESH
            )
    for x in range(1, n_sub):
        pl.semaphore_signal(barrier, inc=1, device_id={"sub": sub ^ x}, device_id_type=MESH)

    low = iota((1, LANES), 1) < HALF
    block0 = seq * rows

    def plan(head):
        o0, o1 = off_ref[0, head], off_ref[1, head]
        m1 = lax.rem(o1, R1)
        late = o0
        second = jnp.where(m1 == o0, lax.rem(o0 + 1, R1), m1)
        third = 0
        for m in reversed(range(R1 - 1)):
            third = jnp.where((late != m) & (second != m), m, third)
        return o0, m1, lax.div(o1, R1), (late, second, third, 6 - late - second - third)

    with jax.named_scope("consts"):
        tok, at = iota((square, square), 0), iota((square, square), 1)
        for odd in range(2):
            hit = tok == at % HALF * R1 + ((at // HALF) ^ odd)
            perm[odd] = jnp.where(hit, 1.0, 0.0).astype(BF)
        at_l, at_j = iota((square, LANES), 0), iota((square, LANES), 1)
        for a in range(R1):
            for half in range(2):
                hit = at_l == (at_j - half * HALF) * R1 + a
                sel[a, pl.ds(half * square, square), :] = jnp.where(hit, 1.0, 0.0).astype(BF)
        for copy in small:
            copy.wait()
        limit = valid_ref[0]
        plans = [plan(sub * heads + h) for h in range(heads)]
        tail_one = jnp.where(iota((FP - HS, square), 0) == 0, 1.0, 0.0).astype(BF)
        for h in range(heads):
            tail = pl.ds(h * FP + HS, FP - HS)
            for m in range(R1):
                pq[m, tail, :] = tail_one
            place = block0 + iota((FP - HS, rows), 1)
            first = iota((FP - HS, rows), 0) == 0
            v_aug[tail, :] = jnp.where(first, 1.0, 0.0).astype(BF)
            k_aug[tail, :] = jnp.where(first & (place >= limit), MASKED, 0.0).astype(BF)

    def permuted(lhs_of, store):
        for c in range(rows // (2 * square)):
            outs = [
                mm(lhs_of(pl.ds((2 * c + b) * square, square)), perm[b]) for b in range(2)
            ]
            for m in range(R1):
                half = slice((m // 2) * LANES, (m // 2 + 1) * LANES)
                even, odd = outs[0][:, half], outs[1][:, half]
                if m % 2:
                    even, odd = odd, even
                store(m, slice(c * LANES, (c + 1) * LANES), jnp.where(low, even, odd).astype(BF))

    with jax.named_scope("load"):
        for i, src in enumerate((k_hbm, v_hbm)):
            pltpu.make_async_copy(src, q_ref, in_sem.at[i]).wait()
        w_fetch.start()

        def store_kv(m, lanes, val):
            pk[m, :, lanes] = val[:cols]
            pv[m, :, lanes] = val[cols:]

        permuted(
            lambda t: jnp.concatenate(
                [ref[pl.ds(h * FP, HS), t] for ref in (k_aug, v_aug) for h in range(heads)], axis=0
            ),
            store_kv,
        )
        for h in range(heads):
            o0, m1, a, _ = plans[h]
            feat = pl.ds(h * HS, HS)
            mid[pos, h, pl.ds(0, HS), :] = pk[o0, feat, :]
            mid[pos, h, pl.ds(HS, HS), :] = pv[o0, feat, :]
            both = jnp.concatenate([pk[m1, feat, :], pv[m1, feat, :]], axis=1)
            wide[seq, feat, :] = mm(both, sel[a]).astype(BF)

    with jax.named_scope("barrier"):
        inner = (seq > 0) & (seq < n_seq - 1)

        @pl.when(inner)
        def _():
            pl.semaphore_wait(barrier, n_sub - 1 + 2)

        @pl.when(jnp.logical_not(inner))
        def _():
            pl.semaphore_wait(barrier, n_sub - 1 + 1)

    def wide_copy(origin, rightward):
        target = seq + 1 if rightward else seq - 1
        return pltpu.make_async_remote_copy(
            src_ref=wide.at[origin], dst_ref=wide.at[origin],
            send_sem=wide_send.at[0], recv_sem=wide_recv.at[origin],
            device_id={"seq": target}, device_id_type=MESH,
        )

    def wide_relay(dist):
        @pl.when(seq - dist >= 0)
        def _():
            wide_copy(seq - dist, True).wait_recv()

            @pl.when(seq < n_seq - 1)
            def _():
                wide_copy(seq - dist, True).start()

        @pl.when(seq + dist < n_seq)
        def _():
            wide_copy(seq + dist, False).wait_recv()

            @pl.when(seq > 0)
            def _():
                wide_copy(seq + dist, False).start()

    def mid_copy(origin, h, kind, count=1):
        ref = mid.at[origin, h if count == 1 else pl.ds(h, count)]
        return pltpu.make_async_remote_copy(
            src_ref=ref, dst_ref=ref,
            send_sem=mid_send.at[0], recv_sem=mid_recv.at[kind, max(h - 1, 0)],
            device_id={"seq": group0 + 1 + lax.rem(pos, 2)}, device_id_type=MESH,
        )

    def mid_arrived(origin, kind, heads_of):
        if heads_of == (0, 1):
            mid_copy(origin, 0, kind, 2).wait_recv()
        else:
            for h in heads_of:
                mid_copy(origin, h, kind).wait_recv()

    own_kind = jnp.where(is_host, 1, 0)

    def q_copy():
        return pltpu.make_async_remote_copy(
            src_ref=guest, dst_ref=guest, send_sem=q_sem.at[0], recv_sem=q_sem.at[1],
            device_id={"seq": group0 + partner}, device_id_type=MESH,
        )

    def ret_copy(h, count=1):
        ref = ret.at[h if count == 1 else pl.ds(h, count)]
        return pltpu.make_async_remote_copy(
            src_ref=ref, dst_ref=ref,
            send_sem=ret_send.at[0], recv_sem=ret_recv.at[max(h - 1, 0)],
            device_id={"seq": group0 + partner}, device_id_type=MESH,
        )

    def relay(heads_of):
        mid_arrived(partner, 0, heads_of)
        for h in heads_of:
            mid_copy(partner, h, 2).start()

    @pl.when(seq < n_seq - 1)
    def _():
        wide_copy(seq, True).start()

    @pl.when(seq > 0)
    def _():
        wide_copy(seq, False).start()

    for h in range(3):
        mid_copy(pos, h, own_kind).start()

    spans = {1: (0, 2), 2: (2, 1), 3: (3, 1)}
    direct = 3
    onward = [(bit, x) for bit in bits for x in range(1, n_sub) if not x % (2 * bit)]

    def x_ref(block, group, slab=None):
        if group:
            first, count = spans[group]
            return xl.at[block, pl.ds(first * HS, count * HS)]
        return xg.at[block] if slab is None else xg.at[block, slab - 1]

    def x_copy(ref, held, bit, group):
        return pltpu.make_async_remote_copy(
            src_ref=ref, dst_ref=ref, send_sem=x_send.at[1 if group else 0],
            recv_sem=x_recv.at[(held ^ bit) - 1, group],
            device_id={"sub": sub ^ bit}, device_id_type=MESH,
        )

    def x_start(group, slab=None):
        ref = x_ref(sub, group, slab)
        for bit in (reversed(range(1, n_sub)) if group == direct else bits):
            x_copy(ref, 0, bit, group).start()

    def x_arrived(x, group):
        x_copy(x_ref(sub ^ x, group), 0, x, group).wait_recv()

    def x_forward(group):
        waited = set()
        for bit, x in onward:
            if x not in waited:
                waited.add(x)
                x_arrived(x, group)
            x_copy(x_ref(sub ^ x, group), x, bit, group).start()

    with jax.named_scope("load_q"):
        q_fetch.wait()

        def store_q(m, lanes, val):
            for h in range(heads):
                pq[m, pl.ds(h * FP, HS), lanes] = val[h * HS:(h + 1) * HS]

        permuted(lambda t: q_ref[:, t], store_q)
        for h in range(heads):
            o0 = plans[h][0]
            mq[pl.ds(h * FP, FP), pl.ds(0, phase)] = pq[o0, pl.ds(h * FP, FP), :]

        @pl.when(is_guest)
        def _():
            for h in range(heads):
                guest[pl.ds(h * HS, HS), :] = pq[plans[h][0], pl.ds(h * FP, HS), :]

    @pl.when(is_guest)
    def _():
        mid_copy(pos, 3, own_kind).start()
        q_copy().start()

    with jax.named_scope("prep"):
        for h in range(heads):
            kr[h] = k_aug[pl.ds(h * FP, FP), :].T

    def attend(keys, values, queries, before=None):
        scores = mm(keys, queries)
        peak = jnp.max(scores, axis=0, keepdims=True)
        if before is not None:
            peak = jnp.maximum(peak, before)
        probs = jnp.exp2((scores - peak) * EXP_SCALE).astype(BF)
        return peak, mm(values, probs)

    def finish(peak, out):
        mass = out[HS:HS + 1]
        return out[:HS] * (1.0 / mass), peak * EXP_SCALE + jnp.log(mass) * LOG2E

    def pipeline(jobs, pieces, keys, queries, values, done):
        def score(i, c, peak):
            part = mm(keys(jobs[i], c), queries(jobs[i]))
            scores[i % 2, pl.ds(c * phase, phase), :] = part
            top = jnp.max(part, axis=0, keepdims=True)
            return top if peak is None else jnp.maximum(peak, top)

        peak = None
        for c in range(pieces):
            peak = score(0, c, peak)
        for i, job in enumerate(jobs):
            ahead = acc = None
            for c in range(pieces):
                if i + 1 < len(jobs):
                    ahead = score(i + 1, c, ahead)
                part = scores[i % 2, pl.ds(c * phase, phase), :]
                probs = jnp.exp2((part - peak) * EXP_SCALE).astype(BF)
                out = mm(values(job, c), probs)
                acc = out if acc is None else acc + out
            done(i, job, peak, acc)
            peak = ahead

    def near_done(i, job, peak, acc):
        m, h = job
        out, lse = finish(peak, acc)
        near_o[m, pl.ds(h * HS, HS), :] = out
        near_l[m, pl.ds(h, 1), :] = lse
        for when, mine in ((6, lax.rem(sub, 2) == 1), (8, lax.rem(sub, 2) == 0)):
            if i == when:
                @pl.when(mine)
                def _():
                    wide_relay(1)

                    @pl.when(is_host)
                    def _():
                        mid_copy(pos, 3, own_kind).start()

    with jax.named_scope("near"):
        pipeline(
            [(m, h) for m in range(R1) for h in range(heads)],
            rows // phase,
            lambda job, c: kr[job[1], pl.ds(c * phase, phase), :],
            lambda job: pq[job[0], pl.ds(job[1] * FP, FP), :],
            lambda job, c: v_aug[pl.ds(job[1] * FP, FP), pl.ds(c * phase, phase)],
            near_done,
        )

    def ship(slab, h, val):
        at = pl.ds(h * HS, HS)
        if slab:
            xg[sub, slab - 1, at, :] = val.astype(BF)
        else:
            xl[sub, at, :] = val.astype(BF)

    with jax.named_scope("ship_near"):
        for slab in (2, 3):
            for h in range(heads):
                ship(slab, h, near_o[plans[h][3][slab], pl.ds(h * HS, HS), :])
            x_start(0, slab)

    ones_tail = jnp.where(iota((FP - HS, phase), 0) == 0, 1.0, 0.0).astype(BF)

    def split(lse, width):
        top = jnp.floor(lse * 0.25) * 4.0
        rest = lse - top
        middle = jnp.floor(rest * 64.0) * (1.0 / 64.0)
        r = iota((FP - HS, width), 0)
        low_part = jnp.where(r == 2, rest - middle, jnp.where(r == 3, 1.0, 0.0))
        return jnp.where(r == 0, top, jnp.where(r == 1, middle, low_part))

    def joined(rows_of):
        return rows_of[0:1] + rows_of[1:2] + rows_of[2:3]

    def mid_kv(origin, h):
        o0 = plans[h][0]
        lane = iota((FP - HS, phase), 1)
        at = jnp.where(lax.rem(o0, 2) == 1, lane ^ HALF, lane)
        place = (group0 + origin) * rows + at * R1 + o0
        dead = (iota((FP - HS, phase), 0) == 0) & (place >= limit)
        dead = jnp.where(dead, MASKED, 0.0).astype(BF)
        return (
            jnp.concatenate([mid[origin, h, pl.ds(0, HS), :], dead], axis=0).T,
            jnp.concatenate([mid[origin, h, pl.ds(HS, HS), :], ones_tail], axis=0),
        )

    def mid_stage(origin, slot):
        for h in range(heads):
            at = pl.ds(slot * phase, phase)
            mkr[h, at, :], mv[pl.ds(h * FP, FP), at] = mid_kv(origin, h)

    def mid_pass():
        def done(i, job, peak, acc):
            h, t = job
            at = pl.ds(t * phase, phase)
            mid_m[pl.ds(h, 1), at] = peak
            mid_o[pl.ds(h * FP, FP), at] = acc

        pipeline(
            [(h, t) for h in range(heads) for t in range(2)],
            GROUP - 1,
            lambda job, c: mkr[job[0], pl.ds(c * phase, phase), :],
            lambda job: mq[pl.ds(job[0] * FP, FP), pl.ds(job[1] * phase, phase)],
            lambda job, c: mv[pl.ds(job[0] * FP, FP), pl.ds(c * phase, phase)],
            done,
        )

    def mid_step(origin, heads_of):
        staged = [mid_kv(origin, h) for h in heads_of]
        scored = [
            mm(keys, mq[pl.ds(h * FP, FP), :]) for h, (keys, _) in zip(heads_of, staged)
        ]
        fore = [(mid_m[pl.ds(h, 1), :], mid_o[pl.ds(h * FP, FP), :]) for h in heads_of]
        done = []
        for score, (_, vals), (before, _) in zip(scored, staged, fore):
            peak = jnp.maximum(jnp.max(score, axis=0, keepdims=True), before)
            probs = jnp.exp2((score - peak) * EXP_SCALE).astype(BF)
            done.append((peak, mm(vals, probs)))
        return [
            (peak, out + old * jnp.exp2((before - peak) * EXP_SCALE))
            for (peak, out), (before, old) in zip(done, fore)
        ]

    def hosted(name, steps):
        @pl.when(is_host)
        def _():
            with jax.named_scope(name):
                for step in steps:
                    step()

    def guest_queries():
        q_copy().wait_recv()
        for h in range(heads):
            at = pl.ds(phase, phase)
            mq[pl.ds(h * FP, HS), at] = guest[pl.ds(h * HS, HS), :]
            mq[pl.ds(h * FP + HS, FP - HS), at] = tail_one

    early, later = (0, 1), (2, 3)
    hosted("relay", [lambda: relay(early), lambda: relay(later)])
    with jax.named_scope("wide_relay2"):
        wide_relay(2)
    hosted("mid_stage", [
        lambda: mid_stage(pos, 0),
        lambda: mid_stage(partner, 1),
        lambda: mid_arrived(across, 1, early),
        lambda: mid_arrived(across, 1, later),
        lambda: mid_stage(across, 2),
    ])
    hosted("guest_q", [guest_queries])
    hosted("mid_pass", [mid_pass])
    def mid_last(heads_of):
        mid_arrived(far, 2, heads_of)
        done = mid_step(far, heads_of)
        for h, (peak, out) in zip(heads_of, done):
            o, lse = finish(peak, out)
            feat = pl.ds(h * FP, HS)
            ret[h, pl.ds(0, HS), :] = o[:, phase:].astype(BF)
            ret[h, pl.ds(HS, FP - HS), :] = split(lse[:, phase:], phase).astype(BF)
            ret_copy(h).start()
            fin_o[pl.ds(h * HS, HS), :] = o[:, :phase]
            fin_l[pl.ds(h, 1), :] = lse[:, :phase]

    hosted("mid_last01", [lambda: mid_last(early)])
    hosted("mid_last2", [lambda: mid_last((2,))])
    hosted("mid_last3", [lambda: mid_last((3,))])
    with jax.named_scope("weights"):
        w_fetch.wait()
        for s in range(n_sub):
            @pl.when(sub == s)
            def _():
                mine = slice(s * cols, (s + 1) * cols)
                wt[...] = w_ref[:, mine].T
                wt_last[...] = jnp.concatenate(
                    [w_ref[(d + 1) * cols - HS:(d + 1) * cols, mine] for d in range(n_sub)], axis=0
                ).T
    with jax.named_scope("wide_relay3"):
        for dist in range(3, n_seq):
            wide_relay(dist)

    with jax.named_scope("wide"):
        q_rows = []
        for h in range(heads):
            _, m1, a, _ = plans[h]
            q_h = mm(pq[m1, pl.ds(h * FP, FP), :], sel[a, pl.ds((h % 2) * square, square), :])
            zero = jnp.zeros((FP, LANES), BF)
            q_h = q_h.astype(BF)
            q_rows.append(jnp.concatenate([q_h, zero] if h < 2 else [zero, q_h], axis=1))
        q_wide = jnp.concatenate(q_rows, axis=0)
        keys, values = [], []
        zeros_tail = jnp.zeros((FP - HS - 8, LANES), F32)
        for pr in range(n_seq // 2):
            one, two = [wide[2 * pr + i].astype(F32) for i in range(2)]
            k_pair = jnp.where(low, one, pltpu.roll(two, HALF, 1))
            v_pair = jnp.where(low, pltpu.roll(one, HALF, 1), two)
            k_rows, v_rows = [], []
            for h in range(heads):
                _, m1, a, _ = plans[h]
                lane = iota((FP - HS, LANES), 1)
                row0 = iota((FP - HS, LANES), 0) == 0
                at = lane % HALF * R1 + a
                at = jnp.where(lax.rem(m1, 2) == 1, at ^ HALF, at)
                place = (2 * pr + lane // HALF) * rows + at * R1 + m1
                k_rows += [
                    k_pair[h * HS:(h + 1) * HS],
                    jnp.where(row0 & (place >= limit), MASKED, 0.0),
                ]
                v_rows += [v_pair[h * HS:(h + 1) * HS], jnp.where(row0, 1.0, 0.0)]
            keys.append(jnp.concatenate(k_rows, axis=0).astype(BF).T)
            values.append(jnp.concatenate(v_rows, axis=0).astype(BF))
        peak, out = attend(
            jnp.concatenate(keys, axis=0), jnp.concatenate(values, axis=1), q_wide
        )
        for h in range(heads):
            _, m1, a, _ = plans[h]
            col = slice((h // 2) * LANES, (h // 2 + 1) * LANES)
            o_h, lse = finish(peak[:, col], out[h * FP:(h + 1) * FP, col])
            z = jnp.concatenate([o_h, split(lse, LANES)], axis=0).astype(BF)
            put = mm_t(z, sel[a, pl.ds((h % 2) * square, square), :])
            spread[pl.ds(h * FP, HS), :] = put[:HS]
            lse = joined(put[HS:])
            lse = jnp.where(put[HS + 3:HS + 4] > 0.5, lse, MASKED)
            spread[pl.ds(h * FP + HS, 8), :] = jnp.broadcast_to(lse, (8, phase))
            two = plans[h][3][1]
            feat = pl.ds(h * HS, HS)
            lse = jnp.where(two == m1, lse, MASKED)
            ship(1, h, combine([
                (near_o[two, feat, :], near_l[two, pl.ds(h, 1), :]), (put[:HS], lse),
            ]))
        x_start(0, 1)

    def returned(heads_of):
        if heads_of == (0, 1):
            ret_copy(0, 2).wait_recv()
        else:
            ret_copy(heads_of[0]).wait_recv()
        for h in heads_of:
            fin_o[pl.ds(h * HS, HS), :] = ret[h, pl.ds(0, HS), :].astype(F32)
            fin_l[pl.ds(h, 1), :] = joined(ret[h, pl.ds(HS, FP - HS), :].astype(F32))

    def conclude(heads_of):
        for h in heads_of:
            o0, m1 = plans[h][:2]
            feat = pl.ds(h * HS, HS)
            lse_w = spread[pl.ds(h * FP + HS, 1), :]
            ship(0, h, combine([
                (near_o[o0, feat, :], near_l[o0, pl.ds(h, 1), :]),
                (fin_o[feat, :], fin_l[pl.ds(h, 1), :]),
                (spread[pl.ds(h * FP, HS), :], jnp.where(m1 == o0, lse_w, MASKED)),
            ]))

    def guested(name, steps):
        @pl.when(is_guest)
        def _():
            with jax.named_scope(name):
                for step in steps:
                    step()

    guested("back01", [lambda: returned(early)])
    with jax.named_scope("conclude01"):
        conclude(early)
        x_start(1)
    for h in later:
        guested(f"back{h}", [lambda: returned((h,))])
        with jax.named_scope(f"conclude{h}"):
            conclude((h,))
            x_start(h)
    with jax.named_scope("x_fwd"):
        x_forward(0)

    with jax.named_scope("x_wait"):
        passed = {x for _, x in onward}
        for group in range(direct):
            if group:
                x_forward(group)
            for x in range(1, n_sub):
                if x not in passed:
                    x_arrived(x, group)

    every = [plan(i)[3] for i in range(n_sub * heads)]
    zeros_head = jnp.zeros((HS, phase), BF)
    with jax.named_scope("project_most"):
        for m in range(R1):
            parts = []
            for d in range(n_sub):
                for h in range(heads):
                    order = every[d * heads + h]
                    at = jnp.where(order[1] == m, 0, jnp.where(order[2] == m, 1, 2))
                    feat = pl.ds(h * HS, HS)
                    held = xl[d, feat, :] if h < heads - 1 else zeros_head
                    parts.append(jnp.where(order[0] == m, held, xg[d, at, feat, :]))
            near_o[m] = mm(wt[...], jnp.concatenate(parts, axis=0))
    with jax.named_scope("x_last"):
        for x in range(1, n_sub):
            x_arrived(x, direct)

    with jax.named_scope("project"):
        outs = []
        for m in range(R1):
            last = jnp.concatenate([
                jnp.where(
                    every[d * heads + heads - 1][0] == m, xl[d, pl.ds(cols - HS, HS), :], zeros_head
                )
                for d in range(n_sub)
            ], axis=0)
            outs.append((near_o[m] + mm(wt_last[...], last)).astype(BF).astype(F32))
        for c in range(rows // (2 * square)):
            at = slice(c * LANES, (c + 1) * LANES)
            for odd in range(2):
                pieces = [
                    jnp.where(low, outs[2 * i + odd][:, at], outs[2 * i + 1 - odd][:, at])
                    for i in range(2)
                ]
                res = mm_t(jnp.concatenate(pieces, axis=1).astype(BF), perm[odd])
                first = (2 * c + odd) * square
                place = block0 + first + iota((1, square), 1)
                o_ref[:, first:first + square] = jnp.where(place < limit, res, 0.0).astype(BF)

    with jax.named_scope("drain"):
        def sent(ref, sem):
            pltpu.make_async_remote_copy(
                src_ref=ref, dst_ref=ref, send_sem=sem, recv_sem=sem,
                device_id={"sub": sub ^ 1}, device_id_type=MESH,
            ).wait_send()

        @pl.when(inner)
        def _():
            sent(wide, wide_send.at[0])

        @pl.when(jnp.logical_not(inner))
        def _():
            sent(wide.at[0], wide_send.at[0])

        @pl.when(is_host)
        def _():
            sent(mid.at[pl.ds(0, 2)], mid_send.at[0])
            sent(ret, ret_send.at[0])

        @pl.when(is_guest)
        def _():
            sent(mid.at[0], mid_send.at[0])
            q_copy().wait_send()

        sent(xg.at[pl.ds(0, n_sub - 1)], x_send.at[0])
        sent(xl.at[pl.ds(0, n_sub - 1)], x_send.at[1])


def local(n_seq, n_sub, q_heads, k_heads, v_heads, w_out, offsets, valid):
    rows, cols = q_heads.shape
    heads = cols // HS
    phase, strip = rows // R1, rows // R2
    assert heads == 4 and n_sub & (n_sub - 1) == 0 and n_seq % 2 == 0 and strip == HALF
    vmem = pl.BlockSpec(memory_space=pltpu.VMEM)
    pad = heads * FP
    return pl.pallas_call(
        functools.partial(kernel, n_seq, n_sub, heads),
        out_shape=jax.ShapeDtypeStruct((cols, rows), BF),
        in_specs=[pl.BlockSpec(memory_space=pl.ANY)] * 6,
        out_specs=vmem,
        scratch_shapes=[
            pltpu.SMEM(offsets.shape, I32),
            pltpu.SMEM(valid.shape, I32),
            pltpu.VMEM((cols, rows), BF),
            pltpu.VMEM((pad, rows), BF),
            pltpu.VMEM((pad, rows), BF),
            pltpu.VMEM(w_out.shape, BF),
            pltpu.VMEM((cols, w_out.shape[0]), BF),
            pltpu.VMEM((cols, n_sub * HS), BF),
            pltpu.VMEM((2, 2 * LANES, 2 * LANES), BF),
            pltpu.VMEM((R1, 4 * LANES, LANES), BF),
            pltpu.VMEM((heads, rows, FP), BF),
            pltpu.VMEM((R1, pad, phase), BF),
            pltpu.VMEM((R1, cols, phase), BF),
            pltpu.VMEM((R1, cols, phase), BF),
            pltpu.VMEM((n_seq + 1, cols, LANES), BF),
            pltpu.VMEM((GROUP, heads, 2 * HS, phase), BF),
            pltpu.VMEM((cols, phase), BF),
            pltpu.VMEM((pad, 2 * phase), BF),
            pltpu.VMEM((heads, (GROUP - 1) * phase, FP), BF),
            pltpu.VMEM((pad, (GROUP - 1) * phase), BF),
            pltpu.VMEM((heads, FP, phase), BF),
            pltpu.VMEM((cols, phase), F32),
            pltpu.VMEM((8, phase), F32),
            pltpu.VMEM((2, rows, phase), F32),
            pltpu.VMEM((R1, cols, phase), F32),
            pltpu.VMEM((R1, 8, phase), F32),
            pltpu.VMEM((pad, 2 * phase), F32),
            pltpu.VMEM((8, 2 * phase), F32),
            pltpu.VMEM((pad, phase), F32),
            pltpu.VMEM((n_sub, R1 - 1, cols, phase), BF),
            pltpu.VMEM((n_sub, cols, phase), BF),
            pltpu.SemaphoreType.DMA((1,)),
            pltpu.SemaphoreType.DMA((n_seq,)),
            pltpu.SemaphoreType.DMA((1,)),
            pltpu.SemaphoreType.DMA((3, 3)),
            pltpu.SemaphoreType.DMA((2,)),
            pltpu.SemaphoreType.DMA((1,)),
            pltpu.SemaphoreType.DMA((3,)),
            pltpu.SemaphoreType.DMA((2,)),
            pltpu.SemaphoreType.DMA((n_sub - 1, 4)),
            pltpu.SemaphoreType.DMA((6,)),
        ],
        compiler_params=pltpu.CompilerParams(
            collective_id=0, has_side_effects=True, vmem_limit_bytes=54784 * 1024
        ),
    )(q_heads.T, k_heads.T, v_heads.T, w_out, offsets, valid).T


def solution(mesh):
    spread = P(("slides", "seq"), "sub")
    return jax.shard_map(
        functools.partial(local, mesh.shape["seq"], mesh.shape["sub"]),
        mesh=mesh,
        in_specs=(spread, spread, spread, P(), P(), P("slides")),
        out_specs=spread,
        check_vma=False,
    )
```

time: 31.6 us -> 28.6 us (0.905)
  the two profiles are of different devices: /device:TPU:1 before, /device:TPU:21 now
where the time goes in v2:
time: 28.6 us; the launch traced here: 28.5 us
  Pallas kernels  26.4 us (92%)
  local copies, waits for them, and re-layouts  1.42 us (5%)
  between operations  0.67 us (2%)
    pallas_call x1, Pallas kernels, local(): pl.pallas_call(functools.partial(kernel, n_seq, n_sub, heads), out_shape=...  26.4 us
    unnamed x3, local copies, waits for them, and re-layouts  1.42 us

profile of v2, /device:TPU:21, one launch (start us, length us, event | category | flops | bytes accessed | tf_op | source)
XLA Modules:
  0.0 28.5 jit_solution(3114793095824852299)
XLA Ops:
  0.7 0.0 copy-start
  0.7 0.7 %copy-done = s32[2,16]{1,0:T(2,128)S(1)} copy-done((s32[2,16]{1,0:T(2,128)S(1)}, s32[2,16]{1,0:T(2,128)}, u32[]{:S(2)}) %copy-start) | copy-done | bytes 152
  1.3 26.4 %shard_map.64 = bf16[192,1024]{1,0:T(8,128)(2,1)S(1)} custom-call(bf16[192,1024]{1,0:T(8,128)(2,1)} %bitcast.5, bf16[192,1024]{1,0:T(8,128)(2,1)} %bitcast.6, bf16[192,1024]{1,0:T(8,128)(2,1)} %bitcast.7, bf16[768,768]{1,0:T(8,128)(2,1)} %w_hbm.1, s32[2,16]{1,0:T(2,128)S(1)} %copy-done, s32[1]{0:T(128)S(6)} %copy.8.valid_hbm), custom_call_target="tpu_custom_call" | custom-call | tf_op jit(solution)/shard_map/pallas_call | solution.py:671
  27.7 0.7 %copy.9 = bf16[1024,192]{0,1:T(8,128)(2,1)} copy(bf16[1024,192]{0,1:T(8,128)(2,1)S(1)} %bitcast.4) | data formatting | bytes 786432
Async XLA Ops:
  0.7 0.7 %copy-start = (s32[2,16]{1,0:T(2,128)S(1)}, s32[2,16]{1,0:T(2,128)}, u32[]{:S(2)}) copy-start(s32[2,16]{1,0:T(2,128)} %off_hbm.1) | copy-start | bytes 388

commit v3 on v2

--- a/solution.py
+++ b/solution.py
@@ -9,6 +9,7 @@
 
 HS = 48
 FP = 64
+TAIL = 8
 GROUP = 4
 R1 = 4
 R2 = 16
@@ -378,11 +379,11 @@
 
     ones_tail = jnp.where(iota((FP - HS, phase), 0) == 0, 1.0, 0.0).astype(BF)
 
-    def split(lse, width):
+    def split(lse, width, count=FP - HS):
         top = jnp.floor(lse * 0.25) * 4.0
         rest = lse - top
         middle = jnp.floor(rest * 64.0) * (1.0 / 64.0)
-        r = iota((FP - HS, width), 0)
+        r = iota((count, width), 0)
         low_part = jnp.where(r == 2, rest - middle, jnp.where(r == 3, 1.0, 0.0))
         return jnp.where(r == 0, top, jnp.where(r == 1, middle, low_part))
 
@@ -472,7 +473,7 @@
             o, lse = finish(peak, out)
             feat = pl.ds(h * FP, HS)
             ret[h, pl.ds(0, HS), :] = o[:, phase:].astype(BF)
-            ret[h, pl.ds(HS, FP - HS), :] = split(lse[:, phase:], phase).astype(BF)
+            ret[h, pl.ds(HS, TAIL), :] = split(lse[:, phase:], phase, TAIL).astype(BF)
             ret_copy(h).start()
             fin_o[pl.ds(h * HS, HS), :] = o[:, :phase]
             fin_l[pl.ds(h, 1), :] = lse[:, :phase]
@@ -487,9 +488,9 @@
             def _():
                 mine = slice(s * cols, (s + 1) * cols)
                 wt[...] = w_ref[:, mine].T
-                wt_last[...] = jnp.concatenate(
-                    [w_ref[(d + 1) * cols - HS:(d + 1) * cols, mine] for d in range(n_sub)], axis=0
-                ).T
+                wt_last[...] = jnp.concatenate([
+                    w_ref[d * cols + cols // 2:(d + 1) * cols, mine] for d in range(n_sub)
+                ], axis=0).T
     with jax.named_scope("wide_relay3"):
         for dist in range(3, n_seq):
             wide_relay(dist)
@@ -552,7 +553,7 @@
             ret_copy(heads_of[0]).wait_recv()
         for h in heads_of:
             fin_o[pl.ds(h * HS, HS), :] = ret[h, pl.ds(0, HS), :].astype(F32)
-            fin_l[pl.ds(h, 1), :] = joined(ret[h, pl.ds(HS, FP - HS), :].astype(F32))
+            fin_l[pl.ds(h, 1), :] = joined(ret[h, pl.ds(HS, TAIL), :].astype(F32))
 
     def conclude(heads_of):
         for h in heads_of:
@@ -582,16 +583,19 @@
             conclude((h,))
             x_start(h)
     with jax.named_scope("x_fwd"):
-        x_forward(0)
+        for group in range(direct):
+            x_forward(group)
+
+    passed = {x for _, x in onward}
+
+    def x_finish(group):
+        for x in range(1, n_sub):
+            if x not in passed or group == direct:
+                x_arrived(x, group)
 
     with jax.named_scope("x_wait"):
-        passed = {x for _, x in onward}
-        for group in range(direct):
-            if group:
-                x_forward(group)
-            for x in range(1, n_sub):
-                if x not in passed:
-                    x_arrived(x, group)
+        x_finish(0)
+        x_finish(1)
 
     every = [plan(i)[3] for i in range(n_sub * heads)]
     zeros_head = jnp.zeros((HS, phase), BF)
@@ -603,21 +607,21 @@
                     order = every[d * heads + h]
                     at = jnp.where(order[1] == m, 0, jnp.where(order[2] == m, 1, 2))
                     feat = pl.ds(h * HS, HS)
-                    held = xl[d, feat, :] if h < heads - 1 else zeros_head
+                    held = xl[d, feat, :] if h < heads // 2 else zeros_head
                     parts.append(jnp.where(order[0] == m, held, xg[d, at, feat, :]))
             near_o[m] = mm(wt[...], jnp.concatenate(parts, axis=0))
     with jax.named_scope("x_last"):
-        for x in range(1, n_sub):
-            x_arrived(x, direct)
+        x_finish(2)
+        x_finish(direct)
 
     with jax.named_scope("project"):
         outs = []
         for m in range(R1):
             last = jnp.concatenate([
                 jnp.where(
-                    every[d * heads + heads - 1][0] == m, xl[d, pl.ds(cols - HS, HS), :], zeros_head
+                    every[d * heads + h][0] == m, xl[d, pl.ds(h * HS, HS), :], zeros_head
                 )
-                for d in range(n_sub)
+                for d in range(n_sub) for h in range(heads // 2, heads)
             ], axis=0)
             outs.append((near_o[m] + mm(wt_last[...], last)).astype(BF).astype(F32))
         for c in range(rows // (2 * square)):
@@ -681,7 +685,7 @@
             pltpu.VMEM((pad, rows), BF),
             pltpu.VMEM(w_out.shape, BF),
             pltpu.VMEM((cols, w_out.shape[0]), BF),
-            pltpu.VMEM((cols, n_sub * HS), BF),
+            pltpu.VMEM((cols, n_sub * cols // 2), BF),
             pltpu.VMEM((2, 2 * LANES, 2 * LANES), BF),
             pltpu.VMEM((R1, 4 * LANES, LANES), BF),
             pltpu.VMEM((heads, rows, FP), BF),
@@ -694,7 +698,7 @@
             pltpu.VMEM((pad, 2 * phase), BF),
             pltpu.VMEM((heads, (GROUP - 1) * phase, FP), BF),
             pltpu.VMEM((pad, (GROUP - 1) * phase), BF),
-            pltpu.VMEM((heads, FP, phase), BF),
+            pltpu.VMEM((heads, HS + TAIL, phase), BF),
             pltpu.VMEM((cols, phase), F32),
             pltpu.VMEM((8, phase), F32),
             pltpu.VMEM((2, rows, phase), F32),

time: 28.6 us -> 27.5 us (0.962)
  the two profiles are of different devices: /device:TPU:21 before, /device:TPU:1 now
where the time goes in v3:
time: 27.5 us; the launch traced here: 27.3 us
  Pallas kernels  25.2 us (92%)
  local copies, waits for them, and re-layouts  1.42 us (5%)
  between operations  0.67 us (2%)
    pallas_call x1, Pallas kernels, local(): pl.pallas_call(functools.partial(kernel, n_seq, n_sub, heads), out_shape=...  25.2 us
    unnamed x3, local copies, waits for them, and re-layouts  1.42 us

profile of v3, /device:TPU:1, one launch (start us, length us, event | category | flops | bytes accessed | tf_op | source)
XLA Modules:
  0.0 27.3 jit_solution(13705351700253546953)
XLA Ops:
  0.7 0.0 copy-start
  0.7 0.7 %copy-done = s32[2,16]{1,0:T(2,128)S(1)} copy-done((s32[2,16]{1,0:T(2,128)S(1)}, s32[2,16]{1,0:T(2,128)}, u32[]{:S(2)}) %copy-start) | copy-done | bytes 152
  1.3 25.2 %shard_map.64 = bf16[192,1024]{1,0:T(8,128)(2,1)S(1)} custom-call(bf16[192,1024]{1,0:T(8,128)(2,1)} %bitcast.5, bf16[192,1024]{1,0:T(8,128)(2,1)} %bitcast.6, bf16[192,1024]{1,0:T(8,128)(2,1)} %bitcast.7, bf16[768,768]{1,0:T(8,128)(2,1)} %w_hbm.1, s32[2,16]{1,0:T(2,128)S(1)} %copy-done, s32[1]{0:T(128)S(6)} %copy.8.valid_hbm), custom_call_target="tpu_custom_call" | custom-call | tf_op jit(solution)/shard_map/pallas_call | solution.py:675
  26.6 0.7 %copy.9 = bf16[1024,192]{0,1:T(8,128)(2,1)} copy(bf16[1024,192]{0,1:T(8,128)(2,1)S(1)} %bitcast.4) | data formatting | bytes 786432
Async XLA Ops:
  0.7 0.7 %copy-start = (s32[2,16]{1,0:T(2,128)S(1)}, s32[2,16]{1,0:T(2,128)}, u32[]{:S(2)}) copy-start(s32[2,16]{1,0:T(2,128)} %off_hbm.1) | copy-start | bytes 388

commit v4 on v3

--- a/solution.py
+++ b/solution.py
@@ -46,7 +46,7 @@
     n_seq, n_sub, heads,
     q_hbm, k_hbm, v_hbm, w_hbm, off_hbm, valid_hbm, o_ref,
     off_ref, valid_ref,
-    q_ref, k_aug, v_aug, w_ref, wt, wt_last,
+    q_ref, k_aug, v_aug, w_ref, wt,
     perm, sel, kr, pq, pk, pv, wide, mid,
     guest, mq, mkr, mv, ret, fin_o, fin_l,
     scores, near_o, near_l, mid_o, mid_m, spread, xg, xl,
@@ -488,9 +488,6 @@
             def _():
                 mine = slice(s * cols, (s + 1) * cols)
                 wt[...] = w_ref[:, mine].T
-                wt_last[...] = jnp.concatenate([
-                    w_ref[d * cols + cols // 2:(d + 1) * cols, mine] for d in range(n_sub)
-                ], axis=0).T
     with jax.named_scope("wide_relay3"):
         for dist in range(3, n_seq):
             wide_relay(dist)
@@ -582,10 +579,6 @@
         with jax.named_scope(f"conclude{h}"):
             conclude((h,))
             x_start(h)
-    with jax.named_scope("x_fwd"):
-        for group in range(direct):
-            x_forward(group)
-
     passed = {x for _, x in onward}
 
     def x_finish(group):
@@ -593,9 +586,16 @@
             if x not in passed or group == direct:
                 x_arrived(x, group)
 
-    with jax.named_scope("x_wait"):
+    def x_pass_late(parity):
+        @pl.when(lax.rem(sub, 2) == parity)
+        def _():
+            for group in range(1, direct):
+                x_forward(group)
+
+    with jax.named_scope("x_fwd"):
+        x_forward(0)
+        x_pass_late(1)
         x_finish(0)
-        x_finish(1)
 
     every = [plan(i)[3] for i in range(n_sub * heads)]
     zeros_head = jnp.zeros((HS, phase), BF)
@@ -607,12 +607,12 @@
                     order = every[d * heads + h]
                     at = jnp.where(order[1] == m, 0, jnp.where(order[2] == m, 1, 2))
                     feat = pl.ds(h * HS, HS)
-                    held = xl[d, feat, :] if h < heads // 2 else zeros_head
-                    parts.append(jnp.where(order[0] == m, held, xg[d, at, feat, :]))
+                    parts.append(jnp.where(order[0] == m, zeros_head, xg[d, at, feat, :]))
             near_o[m] = mm(wt[...], jnp.concatenate(parts, axis=0))
     with jax.named_scope("x_last"):
-        x_finish(2)
-        x_finish(direct)
+        x_pass_late(0)
+        for group in range(1, direct + 1):
+            x_finish(group)
 
     with jax.named_scope("project"):
         outs = []
@@ -621,9 +621,9 @@
                 jnp.where(
                     every[d * heads + h][0] == m, xl[d, pl.ds(h * HS, HS), :], zeros_head
                 )
-                for d in range(n_sub) for h in range(heads // 2, heads)
+                for d in range(n_sub) for h in range(heads)
             ], axis=0)
-            outs.append((near_o[m] + mm(wt_last[...], last)).astype(BF).astype(F32))
+            outs.append((near_o[m] + mm(wt[...], last)).astype(BF).astype(F32))
         for c in range(rows // (2 * square)):
             at = slice(c * LANES, (c + 1) * LANES)
             for odd in range(2):
@@ -685,7 +685,6 @@
             pltpu.VMEM((pad, rows), BF),
             pltpu.VMEM(w_out.shape, BF),
             pltpu.VMEM((cols, w_out.shape[0]), BF),
-            pltpu.VMEM((cols, n_sub * cols // 2), BF),
             pltpu.VMEM((2, 2 * LANES, 2 * LANES), BF),
             pltpu.VMEM((R1, 4 * LANES, LANES), BF),
             pltpu.VMEM((heads, rows, FP), BF),

time: 27.5 us -> 27.1 us (0.985)
  Pallas kernels: 25.2 us -> 24.9 us
    pallas_call x1, Pallas kernels: 25.2 us -> 24.9 us  [local(): pl.pallas_call(functools.partial(kernel, n_seq, n_sub, heads), out_shape=...]
where the time goes in v4:
time: 27.1 us; the launch traced here: 27 us
  Pallas kernels  24.9 us (92%)
  local copies, waits for them, and re-layouts  1.42 us (5%)
  between operations  0.67 us (2%)
    pallas_call x1, Pallas kernels, local(): pl.pallas_call(functools.partial(kernel, n_seq, n_sub, heads), out_shape=...  24.9 us
    unnamed x3, local copies, waits for them, and re-layouts  1.42 us

profile of v4, /device:TPU:1, one launch (start us, length us, event | category | flops | bytes accessed | tf_op | source)
XLA Modules:
  0.0 27.0 jit_solution(3263703254298400676)
XLA Ops:
  0.7 0.0 copy-start
  0.7 0.7 %copy-done = s32[2,16]{1,0:T(2,128)S(1)} copy-done((s32[2,16]{1,0:T(2,128)S(1)}, s32[2,16]{1,0:T(2,128)}, u32[]{:S(2)}) %copy-start) | copy-done | bytes 152
  1.3 24.9 %shard_map.64 = bf16[192,1024]{1,0:T(8,128)(2,1)S(1)} custom-call(bf16[192,1024]{1,0:T(8,128)(2,1)} %bitcast.5, bf16[192,1024]{1,0:T(8,128)(2,1)} %bitcast.6, bf16[192,1024]{1,0:T(8,128)(2,1)} %bitcast.7, bf16[768,768]{1,0:T(8,128)(2,1)} %w_hbm.1, s32[2,16]{1,0:T(2,128)S(1)} %copy-done, s32[1]{0:T(128)S(6)} %copy.8.valid_hbm), custom_call_target="tpu_custom_call" | custom-call | tf_op jit(solution)/shard_map/pallas_call | solution.py:675
  26.2 0.7 %copy.9 = bf16[1024,192]{0,1:T(8,128)(2,1)} copy(bf16[1024,192]{0,1:T(8,128)(2,1)S(1)} %bitcast.4) | data formatting | bytes 786432
Async XLA Ops:
  0.7 0.7 %copy-start = (s32[2,16]{1,0:T(2,128)S(1)}, s32[2,16]{1,0:T(2,128)}, u32[]{:S(2)}) copy-start(s32[2,16]{1,0:T(2,128)} %off_hbm.1) | copy-start | bytes 388
